TPU v7x, 32 devices: a whole 2x2x4 slice. The times are simulated.
32 devices in a mesh: fsdp: 8 (over y, x, core), dp: 4 (over z).
Axes of the slice: x: 2, y: 2, z: 4, core: 2. Of those that a mesh axis runs over, the one named last changes fastest.
Arguments:
- hidden: bfloat16 [8192, 14336], P(('fsdp', 'dp')), may hold values from -6 to 6
- cotangent: bfloat16 [8192, 4096], P(('fsdp', 'dp')), may hold values from -6 to 6
- tiles: bfloat16 [64, 128, 128], P('fsdp'), may hold values from -0.25 to 0.25
- tile_rows: int32 [64], P('fsdp'), may hold values from 0 to 111, as said below
- tile_cols: int32 [64], P('fsdp'), may hold values from 0 to 31, as said below
- counts: int32 [8], P('fsdp'), may hold values from 1 to 8, as said below
Outputs:
- layer_out: bfloat16 [8192, 4096], P(('fsdp', 'dp'))
- hidden_grad: bfloat16 [8192, 14336], P(('fsdp', 'dp'))
- weight_grad: float32 [64, 128, 128], P('fsdp')
Inputs may be any that keep to these rules, and one draw needn't show every extreme that they name: `tile_rows`: every slot (live or not) names a different block; the row block is below 112. `tile_cols`: the column block is below 32. `counts`: some owner has all 8 slots live in every draw.
All inputs are finite; a program needn't handle non-finite values.
Results may differ from a plain program's by a relative error of at most 0.0085.
Values may be sent and summed in bfloat16 or wider, within the bound.
No kernel may reach another device: no remote copies, remote signals or barrier semaphores. Data moves between devices by JAX's collectives and lax.ppermute only.
A program may use at most 192 MiB of HBM per device.

v0:
```python
import math

import jax
import jax.numpy as jnp
from jax import lax
from jax.sharding import PartitionSpec as P


def one_hot_of(ids, width):
    return (ids[:, None] == jnp.arange(width, dtype=jnp.int32)[None, :]).astype(jnp.bfloat16)


def select_blocks(blocks, ids):
    table = one_hot_of(ids, blocks.shape[1])
    chosen = jnp.einsum("tbe,kb->tke", blocks, table, preferred_element_type=jnp.float32)
    return chosen.astype(jnp.bfloat16)


def place_blocks(partial_value, ids, width):
    table = one_hot_of(ids, width).astype(jnp.float32)
    return jnp.einsum("tke,kb->tbe", partial_value, table)


def shards(hidden, cotangent, tiles, tile_rows, tile_cols, counts):
    tokens = hidden.shape[0]
    slots_own = tiles.shape[0]
    edge_len = tiles.shape[1]
    blocks_ff = hidden.shape[1] // edge_len
    blocks_model = cotangent.shape[1] // edge_len
    live_slots = jnp.arange(slots_own) < counts[0]
    masked = jnp.where(live_slots[:, None, None], tiles, jnp.zeros_like(tiles))
    all_rows, all_cols = (
        lax.all_gather(tile_rows, "fsdp", axis=0, tiled=True),
        lax.all_gather(tile_cols, "fsdp", axis=0, tiled=True),
    )
    hidden_blocks = hidden.reshape(tokens, blocks_ff, edge_len)
    upstream_blocks = cotangent.reshape(tokens, blocks_model, edge_len)
    gathered = lax.all_gather(masked, "fsdp", axis=0, tiled=True)
    row_ids = all_rows
    col_ids = all_cols
    picked = select_blocks(hidden_blocks, row_ids)
    partial_value = jnp.einsum("tkf,kfd->tkd", picked, gathered, preferred_element_type=jnp.float32)
    layer_acc = place_blocks(partial_value, col_ids, blocks_model)
    row_ids = all_rows
    col_ids = all_cols
    upstream = select_blocks(upstream_blocks, col_ids)
    partial_value = jnp.einsum(
        "tkd,kfd->tkf", upstream, gathered, preferred_element_type=jnp.float32
    )
    grad_acc = place_blocks(partial_value, row_ids, blocks_ff)
    row_ids = all_rows
    col_ids = all_cols
    picked = select_blocks(hidden_blocks, row_ids)
    upstream = select_blocks(upstream_blocks, col_ids)
    owned = lax.psum_scatter(
        jnp.einsum("tkf,tkd->kfd", picked, upstream, preferred_element_type=jnp.float32),
        "fsdp",
        scatter_dimension=0,
        tiled=True,
    )
    summed = lax.psum(owned, "dp")
    raw_grad = jnp.where(live_slots[:, None, None], summed, jnp.zeros_like(summed))
    local_squares = jnp.sum(raw_grad * raw_grad)
    local_entries = counts[0].astype(jnp.float32) * edge_len * edge_len
    squares, entries = lax.psum((local_squares, local_entries), "fsdp")
    spread = jnp.sqrt(squares / entries)
    root_tokens = math.sqrt(tokens * lax.axis_size("fsdp") * lax.axis_size("dp"))
    factor = jnp.minimum(1.0, 0.5 * root_tokens / spread) / root_tokens
    layer_out = layer_acc.reshape(tokens, blocks_model * edge_len).astype(jnp.bfloat16)
    hidden_grad = grad_acc.reshape(tokens, blocks_ff * edge_len).astype(jnp.bfloat16)
    return (layer_out, hidden_grad, raw_grad * factor)


def solution(mesh):
    placed = (
        P(("fsdp", "dp"), None),
        P(("fsdp", "dp"), None),
        P("fsdp", None, None),
        P("fsdp"),
        P("fsdp"),
        P("fsdp"),
    )
    return jax.shard_map(
        shards,
        mesh=mesh,
        in_specs=placed,
        out_specs=(P(("fsdp", "dp"), None), P(("fsdp", "dp"), None), P("fsdp", None, None)),
        check_vma=False,
    )
```

profile of v0, /device:TPU:0, one launch (start us, length us, event | category | flops | bytes accessed | tf_op | source)
XLA Modules:
  0.0 171.5 jit_solution(11835242717945344327)
XLA Ops:
  7.2 0.0 all-gather.2.cloned.1.call-start
  7.9 1.7 %broadcast_select_fusion = bf16[8,128,128]{2,1,0:T(8,128)(2,1)} fusion(bf16[8,128,128]{2,1,0:T(8,128)(2,1)} %param.8, pred[8]{0:T(512)(128)(4,1)S(1)} %iota_compare_fusion.2), kind=kLoop, calls=%fused_computation.16 | loop fusion | flops 131072 | bytes 524296 | tf_op jit(solution)/shard_map/jit(_where)/select_n | solution.py:31
  9.6 0.0 all-gather.2.cloned.1.call-update
  9.6 0.0 reduce-scatter.2.cloned.1.call-start
  9.7 0.0 copy-start.8
  9.7 0.0 copy-start.6
  9.7 0.0 copy-start.7
  9.7 7.8 %copy.16 = bf16[32,8,112,128]{3,2,1,0:T(8,128)(2,1)} copy(bf16[32,8,112,128]{3,1,2,0:T(8,128)(2,1)} %bitcast.50) | data formatting | bytes 14680064
  17.6 0.0 copy-done.8
  17.6 0.6 dynamic-slice
  18.7 0.0 copy-done.6
  18.7 0.2 dynamic-update-slice
  19.0 0.0 copy-done.7
  19.0 0.2 dynamic-update-slice.1
  19.2 9.7 %all-reduce.2 = (s32[64]{0:T(128)S(1)}, s32[64]{0:T(128)S(1)}) all-reduce(s32[64]{0:T(128)S(1)} %dynamic-update-slice.1, s32[64]{0:T(128)S(1)} %dynamic-update-slice), channel_id=1, replica_groups=mesh['fsdp'=8,'dp'=4] {'fsdp'}, use_global_device_ids=true, to_apply=%add.1 | all-reduce | flops 128 | bytes 1024
  28.9 6.4 %convert_bitcast_fusion.1 = bf16[256,64,128]{2,1,0:T(8,128)(2,1)} fusion(bf16[256,112,128]{2,1,0:T(8,128)(2,1)} %bitcast.46, s32[64]{0:T(128)S(1)} %get-tuple-element.3), kind=kOutput, calls=%fused_computation.7 | convolution fusion | flops 471866368 | bytes 11534592 | tf_op jit(solution)/shard_map/tbe,kb->tke/dot_general | solution.py:15
  35.3 0.0 copy-start.5
  35.3 7.1 %copy.11 = bf16[256,64,128]{0,2,1:T(8,128)(2,1)} copy(bf16[256,64,128]{2,1,0:T(8,128)(2,1)} %convert_bitcast_fusion.1) | data formatting | bytes 8388608 | tf_op jit(solution)/shard_map/convert_element_type | solution.py:16
  42.3 0.0 copy-done.5
  42.3 0.5 copy.18
  42.8 0.0 copy-start
  42.8 1.3 convert_bitcast_fusion
  44.1 0.0 copy-start.1
  44.1 2.0 %copy-done.1 = bf16[256,64,128]{2,1,0:T(8,128)(2,1)} copy-done((bf16[256,64,128]{2,1,0:T(8,128)(2,1)}, bf16[256,64,128]{2,1,0:T(8,128)(2,1)S(1)}, u32[]{:S(2)}) %copy-start.1) | copy-done | bytes 4194328
  46.1 0.0 copy-done
  46.1 7.2 %fusion.9 = f32[64,128,128]{2,1,0:T(8,128)} fusion(bf16[256,64,128]{0,2,1:T(8,128)(2,1)S(1)} %copy-done, bf16[256,64,128]{2,1,0:T(8,128)(2,1)S(1)} %convert_bitcast_fusion), kind=kOutput, calls=%fused_computation.10 | convolution fusion | flops 536870912 | bytes 12582912 | tf_op jit(solution)/shard_map/tkf,tkd->kfd/dot_general | solution.py:56
  53.3 0.0 reduce-scatter.2.cloned.1.call-update
  53.4 0.2 all-reduce.6.cloned.1.call-start
  53.6 0.0 all-gather.2.cloned.1.call-done
  53.6 9.4 %fusion.7 = bf16[64,128,256]{2,1,0:T(8,128)(2,1)} fusion(bf16[64,128,128]{2,1,0:T(8,128)(2,1)} %all-gather.2.cloned.1.call-done, bf16[256,64,128]{2,1,0:T(8,128)(2,1)} %copy-done.1), kind=kOutput, calls=%fused_computation.8 | convolution fusion | flops 536870912 | bytes 10485760 | tf_op jit(solution)/shard_map/tkd,kfd->tkf/dot_general | solution.py:47
  63.0 6.6 %copy.15 = bf16[64,128,256]{1,0,2:T(8,128)(2,1)} copy(bf16[64,128,256]{2,1,0:T(8,128)(2,1)} %fusion.7) | data formatting | bytes 8388608 | tf_op jit(solution)/shard_map/tkd,kfd->tkf/dot_general | solution.py:47
  69.7 0.0 copy-start.3
  69.7 7.6 %fusion.4 = bf16[112,256,128]{2,0,1:T(8,128)(2,1)} fusion(bf16[64,128,256]{1,0,2:T(8,128)(2,1)} %copy.15, s32[64]{0:T(128)S(1)} %get-tuple-element.3), kind=kOutput, calls=%fused_computation.5 | convolution fusion | flops 469769216 | bytes 11534592 | tf_op jit(solution)/shard_map/tke,kb->tbe/dot_general | solution.py:21
  77.3 26.8 %reduce-scatter.2.cloned.1.call-done = f32[8,128,128]{2,1,0:T(8,128)} async-done(((f32[64,128,128]{2,1,0:T(8,128)}), f32[8,128,128]{2,1,0:T(8,128)}) %reduce-scatter.2.cloned.1.call-update) | async-done | bytes 524304 | tf_op jit(solution)/shard_map/reduce_scatter | solution.py:55
  104.1 0.0 all-reduce.6.cloned.1.call-update
  104.1 0.0 copy-done.3
  104.1 0.0 copy-start.2
  104.1 5.6 %fusion.24 = bf16[64,128,256]{2,1,0:T(8,128)(2,1)} fusion(bf16[64,128,128]{2,1,0:T(8,128)(2,1)S(1)} %copy-done.3, bf16[256,64,128]{0,2,1:T(8,128)(2,1)} %copy.11), kind=kOutput, calls=%fused_computation.26 | convolution fusion | flops 536870912 | bytes 10485760 | tf_op jit(solution)/shard_map/tkf,kfd->tkd/dot_general | solution.py:42
  109.8 0.0 copy-done.2
  109.8 4.9 %copy.26 = bf16[32,8,112,128]{3,1,2,0:T(8,128)(2,1)} copy(bf16[32,8,112,128]{3,2,1,0:T(8,128)(2,1)S(1)} %bitcast.47) | data formatting | bytes 14680064
  114.7 6.5 %copy.13 = bf16[64,128,256]{1,0,2:T(8,128)(2,1)} copy(bf16[64,128,256]{2,1,0:T(8,128)(2,1)} %fusion.24) | data formatting | bytes 8388608 | tf_op jit(solution)/shard_map/tkf,kfd->tkd/dot_general | solution.py:42
  121.2 2.9 %fusion.11 = bf16[32,256,128]{2,0,1:T(8,128)(2,1)S(1)} fusion(bf16[64,128,256]{1,0,2:T(8,128)(2,1)} %copy.13, s32[64]{0:T(128)S(1)} %get-tuple-element.4), kind=kOutput, calls=%fused_computation.13 | convolution fusion | flops 134219776 | bytes 6291712 | tf_op jit(solution)/shard_map/tke,kb->tbe/dot_general | solution.py:21
  124.1 21.0 %all-reduce.6.cloned.1.call-done = f32[8,128,128]{2,1,0:T(8,128)} async-done(((f32[8,128,128]{2,1,0:T(8,128)}), f32[8,128,128]{2,1,0:T(8,128)}) %all-reduce.6.cloned.1.call-update) | async-done | bytes 524304 | tf_op jit(solution)/shard_map/psum | solution.py:61
  145.2 1.9 %multiply_reduce_fusion = f32[]{:T(128)} fusion(f32[8,128,128]{2,1,0:T(8,128)} %all-reduce.6.cloned.1.call-done, pred[8]{0:T(512)(128)(4,1)S(1)} %iota_compare_fusion.2), kind=kLoop, calls=%fused_computation.14 | loop fusion | flops 393215 | bytes 524300 | tf_op jit(solution)/shard_map/reduce_sum | solution.py:63
  147.1 2.3 %copy.27 = bf16[32,8,32,128]{3,1,2,0:T(8,128)(2,1)} copy(bf16[32,8,32,128]{3,2,1,0:T(8,128)(2,1)S(1)} %bitcast.48) | data formatting | bytes 4194304
  149.4 13.3 %all-reduce.3 = (f32[]{:T(128)}, f32[]{:T(128)}) all-reduce(f32[]{:T(128)} %multiply_reduce_fusion, f32[]{:T(128)S(6)} %mul.14), channel_id=1, replica_groups=mesh['fsdp'=8,'dp'=4] {'fsdp'}, use_global_device_ids=true, to_apply=%region_3.4 | all-reduce | flops 2 | bytes 16 | tf_op jit(solution)/shard_map/psum | solution.py:65
  164.0 0.0 copy-done.4
  164.0 0.9 select_multiply_fusion
  (4 shorter events, 0.0 us)
Async XLA Ops:
  7.2 46.5 %all-gather.2.cloned.1.call-start = ((), (), s32[]{:S(2)}) async-start(), calls=%async_computation.1 | async-start | bytes 2359296 | tf_op jit(solution)/shard_map/all_gather | solution.py:38
  9.6 94.5 %reduce-scatter.2.cloned.1.call-start = ((), (), s32[]{:S(2)}) async-start(), calls=%async_computation.2 | async-start | bytes 4718592 | tf_op jit(solution)/shard_map/reduce_scatter | solution.py:55
  9.7 7.9 %copy-start.8 = (u32[32]{0:T(128)S(1)}, u32[32]{0:T(128)}, u32[]{:S(2)}) copy-start(u32[32]{0:T(128)} %constant.18) | copy-start | bytes 388
  9.7 9.0 %copy-start.6 = (s32[8]{0:T(128)S(1)}, s32[8]{0:T(128)}, u32[]{:S(2)}) copy-start(s32[8]{0:T(128)} %param.10) | copy-start | bytes 100
  9.7 9.3 %copy-start.7 = (s32[8]{0:T(128)S(1)}, s32[8]{0:T(128)}, u32[]{:S(2)}) copy-start(s32[8]{0:T(128)} %param.9) | copy-start | bytes 100
  35.3 7.1 %copy-start.5 = (bf16[256,4096]{1,0:T(8,128)(2,1)S(1)}, bf16[256,4096]{1,0:T(8,128)(2,1)}, u32[]{:S(2)}) copy-start(bf16[256,4096]{1,0:T(8,128)(2,1)} %param.7) | copy-start | bytes 6291460
  42.8 3.3 %copy-start = (bf16[256,64,128]{0,2,1:T(8,128)(2,1)S(1)}, bf16[256,64,128]{0,2,1:T(8,128)(2,1)}, u32[]{:S(2)}) copy-start(bf16[256,64,128]{0,2,1:T(8,128)(2,1)} %copy.11) | copy-start | bytes 12582916
  44.1 2.0 %copy-start.1 = (bf16[256,64,128]{2,1,0:T(8,128)(2,1)}, bf16[256,64,128]{2,1,0:T(8,128)(2,1)S(1)}, u32[]{:S(2)}) copy-start(bf16[256,64,128]{2,1,0:T(8,128)(2,1)S(1)} %convert_bitcast_fusion) | copy-start | bytes 12582916
  53.4 91.8 %all-reduce.6.cloned.1.call-start = ((), (), s32[]{:S(2)}) async-start(), calls=%async_computation.3 | async-start | bytes 1048576 | tf_op jit(solution)/shard_map/psum | solution.py:61
  69.7 34.5 %copy-start.3 = (bf16[64,128,128]{2,1,0:T(8,128)(2,1)S(1)}, bf16[64,128,128]{2,1,0:T(8,128)(2,1)}, u32[]{:S(2)}) copy-start(bf16[64,128,128]{2,1,0:T(8,128)(2,1)} %all-gather.2.cloned.1.call-done) | copy-start | bytes 6291460
  104.1 5.6 %copy-start.2 = (bf16[112,256,128]{2,0,1:T(8,128)(2,1)S(1)}, bf16[112,256,128]{2,0,1:T(8,128)(2,1)}, u32[]{:S(2)}) copy-start(bf16[112,256,128]{2,0,1:T(8,128)(2,1)} %fusion.4) | copy-start | bytes 22020100
  145.2 18.9 %copy-start.4 = (f32[8,128,128]{2,1,0:T(8,128)S(1)}, f32[8,128,128]{2,1,0:T(8,128)}, u32[]{:S(2)}) copy-start(f32[8,128,128]{2,1,0:T(8,128)} %all-reduce.6.cloned.1.call-done) | copy-start | bytes 1572868
Sparse Core Ops, SparseCore 0:
  10.4 30.5 all-gather.1
  53.5 50.5 reduce-scatter.1
  106.4 38.6 all-reduce.5
where the time goes:
time: 172 us; the launch traced here: 171 us
  waiting for transfers between devices  47.9 us (28%)
  matrix products  40.4 us (23%)
  local copies, waits for them, and re-layouts  38.9 us (23%)
  blocking collectives  23 us (13%)
  between operations  16.4 us (10%)
  other arithmetic  4.57 us (3%)
    reduce_scatter x1, waiting for transfers between devices, shards(): lax.psum_scatter(jnp.einsum('tkf,tkd->kfd', picked, upstream, preferred_e...  26.8 us
    psum x1, waiting for transfers between devices, shards(): summed = lax.psum(owned, 'dp')  21 us
    unnamed x27, local copies, waits for them, and re-layouts  18.6 us
    psum x1, blocking collectives, shards(): squares, entries = lax.psum((local_squares, local_entries), 'fsdp')  13.3 us
    dot_general x2, matrix products, place_blocks(): return jnp.einsum('tke,kb->tbe', partial_value, table)  10.5 us
    unnamed x1, blocking collectives  9.69 us
    dot_general x1, matrix products, shards(): jnp.einsum('tkd,kfd->tkf', upstream, gathered, preferred_element_type=jnp...  9.41 us
    dot_general x2, matrix products, select_blocks(): jnp.einsum('tbe,kb->tke', blocks, table, preferred_element_type=jnp.float32)  7.66 us
  transfers between devices with their start and end apart: 3, of which 2 were waited for; matrix products, arithmetic and copies ran while one was open for 44% of the time, Pallas kernels for 0%

commit v1 on v0

v1 whole, which is shorter than its diff:
```python
import functools
import math

import jax
import jax.numpy as jnp
from jax import lax
from jax.experimental import pallas as pl
from jax.experimental.pallas import tpu as pltpu
from jax.sharding import PartitionSpec as P


F32, BF16 = jnp.float32, jnp.bfloat16
VMEM = pl.BlockSpec(memory_space=pltpu.VMEM)
SMEM = pl.BlockSpec(memory_space=pltpu.SMEM)
HBM = pl.BlockSpec(memory_space=pltpu.HBM)
UNROLL = 8
CHUNKS = 1


def shaped(dims, dtype):
    return jax.ShapeDtypeStruct(tuple(dims), dtype)


def kernel_call(body, out_shape, in_specs, out_specs, args, scratch=(), grid=(), limit=8, flops=0, moved=1 << 20):
    return pl.pallas_call(
        body,
        out_shape=out_shape,
        grid=grid,
        in_specs=in_specs,
        out_specs=out_specs,
        scratch_shapes=scratch,
        compiler_params=pltpu.CompilerParams(vmem_limit_bytes=limit << 20),
        cost_estimate=pl.CostEstimate(flops=flops, bytes_accessed=moved, transcendentals=0),
    )(*args)


def swap(value, axis, mask):
    size = lax.axis_size(axis)
    return lax.ppermute(value, axis, [(i, i ^ mask) for i in range(size)])


def lanes(block, edge):
    return pl.ds(pl.multiple_of(block * edge, edge), edge)


def contract(left, right, left_dim, right_dim):
    dims = (((left_dim,), (right_dim,)), ((), ()))
    return lax.dot_general(left, right, dims, preferred_element_type=F32)


def stage_kernel(edge, cotangent, flipped):
    def step(i, carry):
        for u in range(UNROLL):
            block = i * UNROLL + u
            flipped[block] = cotangent[:, lanes(block, edge)].T
        return carry

    lax.fori_loop(0, flipped.shape[0] // UNROLL, step, 0)


def terms_kernel(slots, edge, span, flipped, hidden, *refs):
    mine, theirs, where, rows, cols = refs[-5:]
    metas = refs[:-5]
    width = mine.shape[1]
    for parity, target in ((0, mine), (1, theirs)):
        target[...] = jnp.zeros(target.shape, target.dtype)

        end = jnp.int32(0)
        for pair, meta in enumerate(metas):
            for j in span:
                where[end] = pair * width + (j - span[0])
                rows[end] = meta[parity, j]
                cols[end] = meta[parity, slots + j]
                end = end + (j < meta[parity, 2 * slots]).astype(jnp.int32)
        last = jnp.maximum(end - 1, 0)
        for u in range(UNROLL - 1):
            where[end + u] = where[last]
            rows[end + u] = rows[last]
            cols[end + u] = cols[last]

        def step(i, carry):
            for u in range(UNROLL):
                at = i * UNROLL + u
                term = contract(flipped[cols[at]], hidden[:, lanes(rows[at], edge)], 1, 0)
                spot = where[at]
                target[spot // width, spot % width] = term.astype(target.dtype)
            return carry

        lax.fori_loop(0, (end + UNROLL - 1) // UNROLL, step, 0)


def on_chip_kernel(mine, arrived, own, *sent):
    own[...] = mine[0] + arrived[0].astype(F32)
    for m, out in enumerate(sent):
        out[...] = (mine[m + 1] + arrived[m + 1].astype(F32)).astype(BF16)


def in_plane_kernel(share, n_dp, *refs):
    parts, outs = refs[:-n_dp], refs[-n_dp:]
    place = lax.axis_index("dp")
    for m, out in enumerate(outs):
        at = pl.ds((place ^ m) * share, share)
        out[...] = pair_sum([ref[at].astype(F32) for ref in parts]).astype(out.dtype)


def settle_kernel(own, *refs):
    arrived, final, squares = refs[:-2], refs[-2], refs[-1]
    total = pair_sum([own[...]] + [ref[...].astype(F32) for ref in arrived])
    squared = jnp.sum(jnp.sum(total * total, axis=0), axis=0, keepdims=True)
    squares[...] = jnp.broadcast_to(squared, squares.shape)
    for i in range(total.shape[0]):
        final[i] = total[i].T.astype(BF16)


def finish_kernel(root_tokens, slots, edge, chunks, pairs, *refs):
    metas, squares, pieces, out = refs[:pairs], refs[pairs : pairs + chunks], refs[pairs + chunks : -1], refs[-1]
    place = lax.axis_index("dp")
    live = 0
    for meta in metas:
        live = live + meta[0, 2 * slots] + meta[1, 2 * slots]
    entries = live.astype(F32) * (edge * edge)
    total = pair_sum([jnp.sum(ref[...], keepdims=True) for ref in squares])
    spread = jnp.sqrt(total / entries)
    factor = jnp.minimum(1.0, 0.5 * root_tokens / spread) / root_tokens
    per_chunk = len(pieces) // chunks
    for i, piece in enumerate(pieces):
        chunk, m = i // per_chunk, i % per_chunk
        out[chunk * per_chunk + (place ^ m)] = piece[...].astype(F32) * factor[:, :, None]


def products_kernel(slots, edge, out_at, in_at, flip, pairs, source, *refs):
    metas, weights, out = refs[:pairs], refs[pairs : 3 * pairs], refs[3 * pairs]
    held, made, heads, nexts, picks, sources, filled, starts = refs[3 * pairs + 1 :]
    blocks = heads.shape[0] - 1
    group = out.shape[1] // edge

    @pl.when(pl.program_id(0) == 0)
    def _():
        for block in range(blocks):
            heads[block] = -1
        for owner, ref in enumerate(weights):
            held[owner * slots : (owner + 1) * slots] = ref[...]
        at = jnp.int32(0)
        for owner in range(2 * pairs):
            meta, side = metas[owner // 2], owner % 2
            count = meta[side, 2 * slots]
            for j in range(slots):
                block = jnp.where(j < count, meta[side, out_at * slots + j], blocks)
                picks[at] = owner * slots + j
                sources[at] = meta[side, in_at * slots + j]
                nexts[at] = heads[block]
                heads[block] = at
                at = at + (j < count).astype(jnp.int32)
        last = jnp.maximum(at - 1, 0)
        for u in range(UNROLL - 1):
            picks[at + u] = picks[last]
            sources[at + u] = sources[last]

        def step(i, carry):
            for u in range(UNROLL):
                spot = i * UNROLL + u
                left = source[:, lanes(sources[spot], edge)]
                made[spot] = contract(left, held[picks[spot]], 1, 1 if flip else 0)
            return carry

        lax.fori_loop(0, (at + UNROLL - 1) // UNROLL, step, 0)
        at = jnp.int32(0)
        for block in range(blocks):
            if block % group == 0:
                starts[block // group] = at
            filled[at] = block % group
            at = at + (heads[block] >= 0).astype(jnp.int32)
        starts[blocks // group] = at

    turn = pl.program_id(0)
    out[...] = jnp.zeros(out.shape, out.dtype)

    def fill(i, carry):
        first = heads[turn * group + filled[i]]

        def more(s):
            made[first] += made[s]
            return nexts[s]

        lax.while_loop(lambda s: s >= 0, more, nexts[first])
        out[:, lanes(filled[i], edge)] = made[first].astype(out.dtype)
        return carry

    lax.fori_loop(starts[turn], starts[turn + 1], fill, 0)


def products(metas, source, weights, width, slots, edge, flip, steps):
    tokens = source.shape[0]
    blocks = width // edge
    total = len(weights) * slots
    out_at, in_at = (0, 1) if flip else (1, 0)
    return kernel_call(
        functools.partial(products_kernel, slots, edge, out_at, in_at, flip, len(metas)),
        shaped((tokens, width), BF16),
        [VMEM] + [SMEM] * len(metas) + [VMEM] * len(weights),
        pl.BlockSpec((tokens, blocks // steps * edge), lambda i: (0, i)),
        [source] + metas + weights,
        scratch=[
            pltpu.VMEM((total, edge, edge), BF16),
            pltpu.VMEM((total + UNROLL, tokens, edge), F32),
            pltpu.SMEM((blocks + 1,), jnp.int32),
            pltpu.SMEM((total + UNROLL,), jnp.int32),
            pltpu.SMEM((total + UNROLL,), jnp.int32),
            pltpu.SMEM((total + UNROLL,), jnp.int32),
            pltpu.SMEM((blocks + 1,), jnp.int32),
            pltpu.SMEM((steps + 1,), jnp.int32),
        ],
        grid=(steps,),
        limit=24 if total <= 64 else 63,
        flops=1 << 34,
        moved=tokens * width * 2,
    )


def pair_sum(terms):
    while len(terms) > 1:
        terms = [a + b for a, b in zip(terms[::2], terms[1::2])]
    return terms[0]


def shards(hidden, cotangent, tiles, tile_rows, tile_cols, counts):
    n_fsdp, n_dp = lax.axis_size("fsdp"), lax.axis_size("dp")
    tokens = hidden.shape[0]
    slots, edge = tiles.shape[0], tiles.shape[1]
    pairs = n_fsdp // 2
    width = slots // CHUNKS
    share = width // n_dp
    blocks_model = cotangent.shape[1] // edge
    root_tokens = math.sqrt(tokens * n_fsdp * n_dp)
    apart = range(1, pairs)

    filler = jnp.zeros((128 - 2 * slots - 1,), jnp.int32)
    packed = jnp.concatenate([tile_rows, tile_cols, counts, filler])[None]
    near = jnp.concatenate([packed, swap(packed, "fsdp", 1)])
    metas = [near] + [swap(near, "fsdp", 2 * m) for m in apart]

    across = [tiles]
    for m in apart:
        top = 1 << (m.bit_length() - 1)
        across.append(swap(across[m ^ top], "fsdp", 2 * top))
    beside = [swap(across[m], "fsdp", 1) for m in range(pairs)]
    weights = [w for both in zip(across, beside) for w in both]

    flipped = kernel_call(
        functools.partial(stage_kernel, edge),
        shaped((blocks_model, edge, tokens), BF16),
        [VMEM],
        VMEM,
        [cotangent],
        flops=1 << 34,
        moved=4 << 20,
    )

    squares, pieces = [], []
    for c in range(CHUNKS):
        span = range(c * width, (c + 1) * width)
        dims = (pairs, width, edge, edge)
        mine, theirs = kernel_call(
            functools.partial(terms_kernel, slots, edge, span),
            (shaped(dims, F32), shaped(dims, BF16)),
            [VMEM, VMEM] + [SMEM] * pairs,
            (VMEM, VMEM),
            [flipped, hidden] + metas,
            scratch=[pltpu.SMEM((pairs * width + UNROLL,), jnp.int32)] * 3,
            limit=16,
            flops=4 * pairs * width * tokens * edge * edge,
        )
        arrived = swap(theirs, "fsdp", 1)
        own, *sent = kernel_call(
            on_chip_kernel,
            (shaped(dims[1:], F32),) + (shaped(dims[1:], BF16),) * (pairs - 1),
            [VMEM, VMEM],
            (VMEM,) * pairs,
            [mine, arrived],
            flops=1 << 26,
        )
        arrived = [swap(sent[m - 1], "fsdp", 2 * m) for m in apart]
        piece = (share, edge, edge)
        own, *sent = kernel_call(
            functools.partial(in_plane_kernel, share, n_dp),
            (shaped(piece, F32),) + (shaped(piece, BF16),) * (n_dp - 1),
            [VMEM] * pairs,
            (VMEM,) * n_dp,
            [own] + arrived,
            flops=1 << 26,
        )
        arrived = [swap(sent[m - 1], "dp", m) for m in range(1, n_dp)]
        final, squared = kernel_call(
            settle_kernel,
            (shaped(piece, BF16), shaped((n_fsdp * n_dp, edge), F32)),
            [VMEM] * n_dp,
            (VMEM, VMEM),
            [own] + arrived,
            flops=1 << 26,
        )
        pieces += [final] + [swap(final, "dp", m) for m in range(1, n_dp)]
        squares.append(lax.all_to_all(squared, ("fsdp", "dp"), 0, 0, tiled=True))

    hidden_grad = products(metas, cotangent, weights, hidden.shape[1], slots, edge, True, 4)
    layer_out = products(metas, hidden, weights, cotangent.shape[1], slots, edge, False, 2)
    weight_grad = kernel_call(
        functools.partial(finish_kernel, root_tokens, slots, edge, CHUNKS, pairs),
        shaped((CHUNKS * n_dp, share, edge, edge), F32),
        [SMEM] * pairs + [VMEM] * (len(squares) + len(pieces)),
        VMEM,
        metas + squares + pieces,
        flops=1 << 26,
    )
    return layer_out, hidden_grad, weight_grad.reshape(slots, edge, edge)


def solution(mesh):
    placed = (
        P(("fsdp", "dp"), None),
        P(("fsdp", "dp"), None),
        P("fsdp", None, None),
        P("fsdp"),
        P("fsdp"),
        P("fsdp"),
    )
    return jax.shard_map(
        shards,
        mesh=mesh,
        in_specs=placed,
        out_specs=(P(("fsdp", "dp"), None), P(("fsdp", "dp"), None), P("fsdp", None, None)),
        check_vma=False,
    )
```

time: 172 us -> 77.6 us (0.45)
  matrix products: 40.4 us -> 0 us
  local copies, waits for them, and re-layouts: 38.9 us -> 6.64 us
  starting transfers between devices: 0.3 us -> 27.8 us
  waiting for transfers between devices: 47.9 us -> 21.7 us
  blocking collectives: 23 us -> 0 us
  Pallas kernels: 0 us -> 18.9 us
  between operations: 16.4 us -> 1.45 us
  other arithmetic: 4.57 us -> 0.76 us
    dot_general x7 -> x0, matrix products: 40.4 us -> none  [the longest x2 10.5 us: place_blocks(): return jnp.einsum('tke,kb->tbe', partial_value, table)]
    reduce_scatter x1 -> x0, waiting for transfers between devices: 26.8 us -> none  [shards(): lax.psum_scatter(jnp.einsum('tkf,tkd->kfd', picked, upstream, preferred_e...]
    ppermute x0 -> x21, starting transfers between devices: none -> 22.7 us  [swap(): return lax.ppermute(value, axis, [(i, i ^ mask) for i in range(size)])]
    ppermute x0 -> x21, waiting for transfers between devices: none -> 21.7 us  [swap(): return lax.ppermute(value, axis, [(i, i ^ mask) for i in range(size)])]
    psum x1 -> x0, waiting for transfers between devices: 21 us -> none  [shards(): summed = lax.psum(owned, 'dp')]
    pallas_call x0 -> x8, Pallas kernels: none -> 18.9 us  [kernel_call(): pl.pallas_call(body, out_shape=out_shape, grid=grid, in_specs=in_specs, o...]
    psum x1 -> x0, blocking collectives: 13.3 us -> none  [shards(): squares, entries = lax.psum((local_squares, local_entries), 'fsdp')]
    dot_general x2 -> x0, local copies, waits for them, and re-layouts: 13.2 us -> none  [the longest x1 6.63 us: shards(): jnp.einsum('tkd,kfd->tkf', upstream, gathered, preferred_element_type=jnp...]
  transfers between devices with their start and end apart: 3 -> 22, of which waited for: 2 -> 8; matrix products, arithmetic and copies ran while one was open for 44% -> 0% of each run, Pallas kernels for 0% -> 17%
where the time goes in v1:
time: 77.6 us; the launch traced here: 77.2 us
  starting transfers between devices  27.8 us (36%)
  waiting for transfers between devices  21.7 us (28%)
  Pallas kernels  18.9 us (24%)
  local copies, waits for them, and re-layouts  6.64 us (9%)
  between operations  1.45 us (2%)
    ppermute x21, starting transfers between devices, swap(): return lax.ppermute(value, axis, [(i, i ^ mask) for i in range(size)])  22.7 us
    ppermute x21, waiting for transfers between devices, swap(): return lax.ppermute(value, axis, [(i, i ^ mask) for i in range(size)])  21.7 us
    pallas_call x8, Pallas kernels, kernel_call(): pl.pallas_call(body, out_shape=out_shape, grid=grid, in_specs=in_specs, o...  18.9 us
    unnamed x24, local copies, waits for them, and re-layouts  6.64 us
    all_to_all x1, starting transfers between devices, shards(): squares.append(lax.all_to_all(squared, ('fsdp', 'dp'), 0, 0, tiled=True))  5.15 us
  transfers between devices with their start and end apart: 22, of which 8 were waited for; matrix products, arithmetic and copies ran while one was open for 0% of the time, Pallas kernels for 17%

profile of v1, /device:TPU:0, one launch (start us, length us, event | category | flops | bytes accessed | tf_op | source)
XLA Modules:
  0.0 77.2 jit_solution(15873814639241025319)
XLA Ops:
  1.3 0.8 add_bitcast_fusion
  2.0 0.5 collective-permute-start
  2.5 0.8 %collective-permute-done = s32[1,128]{1,0:T(1,128)S(1)} collective-permute-done((s32[1,128]{1,0:T(1,128)S(1)}, s32[1,128]{1,0:T(1,128)S(1)}, u32[]{:S(2)}, u32[]{:S(2)}) %collective-permute-start) | collective-permute-done | bytes 544 | tf_op jit(solution)/shard_map/ppermute | solution.py:39
  3.4 3.8 %collective-permute-start.3 = (s32[2,128]{1,0:T(2,128)S(1)}, s32[2,128]{1,0:T(2,128)S(1)}, u32[]{:S(2)}, u32[]{:S(2)}) collective-permute-start(s32[2,128]{1,0:T(2,128)S(1)} %pad_add_fusion.refs_0_), channel_id=1, source_target_pairs={{0,24},{4,28},{8,16},{12,20},{16,8},{20,12},{24,0},{28,4},{1,25},{... | collective-permute-start | bytes 3080 | tf_op jit(solution)/shard_map/ppermute | solution.py:39
  7.1 0.5 collective-permute-start.2
  7.6 0.1 collective-permute-start.1
  7.8 1.6 %copy-done.1 = bf16[256,4096]{1,0:T(8,128)(2,1)S(1)} copy-done((bf16[256,4096]{1,0:T(8,128)(2,1)S(1)}, bf16[256,4096]{1,0:T(8,128)(2,1)}, u32[]{:S(2)}) %copy-start.1) | copy-done | bytes 2097176
  9.4 0.8 shard_map.87.flipped
  10.1 0.0 copy-start.3
  10.2 0.0 collective-permute-done.3.refs_3_
  10.2 0.5 collective-permute-done.2.refs_2_
  10.7 0.5 collective-permute-done.1.refs_1_
  11.2 1.2 %copy-done = bf16[256,14336]{1,0:T(8,128)(2,1)S(1)} copy-done((bf16[256,14336]{1,0:T(8,128)(2,1)S(1)}, bf16[256,14336]{1,0:T(8,128)(2,1)}, u32[]{:S(2)}) %copy-start) | copy-done | bytes 7340056
  12.4 3.3 %shard_map.88 = (f32[4,8,128,128]{3,2,1,0:T(8,128)S(1)}, bf16[4,8,128,128]{3,2,1,0:T(8,128)(2,1)S(1)}) custom-call(bf16[32,128,256]{2,1,0:T(8,128)(2,1)S(1)} %shard_map.87.flipped, bf16[256,14336]{1,0:T(8,128)(2,1)S(1)} %copy-done, s32[2,128]{1,0:T(2,128)S(1)} %pad_add_fusion.refs_0_, s32[2,128]{1,0:T(2,128)S(1)} %collective-permute-done.1.refs_1_, ...), custom_call_target="tpu_custom_call" | custom-call | flops 536870912 | bytes 1048576 | tf_op jit(solution)/shard_map/pallas_call | solution.py:25
  15.8 0.1 collective-permute-start.11
  15.9 2.0 %collective-permute-start.5 = (bf16[8,128,128]{2,1,0:T(8,128)(2,1)S(1)}, bf16[8,128,128]{2,1,0:T(8,128)(2,1)S(1)}, u32[]{:S(2)}, u32[]{:S(2)}) collective-permute-start(bf16[8,128,128]{2,1,0:T(8,128)(2,1)S(1)} %copy-done.3), channel_id=1, source_target_pairs={{0,8},{4,12},{8,0},{12,4},{16,24},{20,28},{24,16},{28,20},{1,9},{5... | collective-permute-start | bytes 786440 | tf_op jit(solution)/shard_map/ppermute | solution.py:39
  17.8 1.5 %collective-permute-start.7 = (bf16[8,128,128]{2,1,0:T(8,128)(2,1)S(1)}, bf16[8,128,128]{2,1,0:T(8,128)(2,1)S(1)}, u32[]{:S(2)}, u32[]{:S(2)}) collective-permute-start(bf16[8,128,128]{2,1,0:T(8,128)(2,1)S(1)} %copy-done.3), channel_id=1, source_target_pairs={{0,16},{4,20},{8,24},{12,28},{16,0},{20,4},{24,8},{28,12},{1,17},{... | collective-permute-start | bytes 786440 | tf_op jit(solution)/shard_map/ppermute | solution.py:39
  19.3 5.4 %collective-permute-done.5.refs_6_ = bf16[8,128,128]{2,1,0:T(8,128)(2,1)S(1)} collective-permute-done((bf16[8,128,128]{2,1,0:T(8,128)(2,1)S(1)}, bf16[8,128,128]{2,1,0:T(8,128)(2,1)S(1)}, u32[]{:S(2)}, u32[]{:S(2)}) %collective-permute-start.5) | collective-permute-done | bytes 262176 | tf_op jit(solution)/shard_map/ppermute | solution.py:39
  24.7 1.8 %collective-permute-start.9 = (bf16[8,128,128]{2,1,0:T(8,128)(2,1)S(1)}, bf16[8,128,128]{2,1,0:T(8,128)(2,1)S(1)}, u32[]{:S(2)}, u32[]{:S(2)}) collective-permute-start(bf16[8,128,128]{2,1,0:T(8,128)(2,1)S(1)} %collective-permute-done.5.refs_6_), channel_id=1, source_target_pairs={{0,16},{4,20},{8,24},{12,28},{16,0},{20,4},{24,8},{28,12},{1,17},{... | collective-permute-start | bytes 786440 | tf_op jit(solution)/shard_map/ppermute | solution.py:39
  26.5 0.2 shard_map.89
  26.7 1.6 %collective-permute-start.12 = (bf16[8,128,128]{2,1,0:T(8,128)(2,1)S(1)}, bf16[8,128,128]{2,1,0:T(8,128)(2,1)S(1)}, u32[]{:S(2)}, u32[]{:S(2)}) collective-permute-start(bf16[8,128,128]{2,1,0:T(8,128)(2,1)S(1)} %get-tuple-element.18), channel_id=1, source_target_pairs={{0,8},{4,12},{8,0},{12,4},{16,24},{20,28},{24,16},{28,20},{1,9},{5... | collective-permute-start | bytes 786440 | tf_op jit(solution)/shard_map/ppermute | solution.py:39
  28.2 0.5 collective-permute-start.13
  28.7 1.5 %collective-permute-start.14 = (bf16[8,128,128]{2,1,0:T(8,128)(2,1)S(1)}, bf16[8,128,128]{2,1,0:T(8,128)(2,1)S(1)}, u32[]{:S(2)}, u32[]{:S(2)}) collective-permute-start(bf16[8,128,128]{2,1,0:T(8,128)(2,1)S(1)} %get-tuple-element.20), channel_id=1, source_target_pairs={{0,24},{4,28},{8,16},{12,20},{16,8},{20,12},{24,0},{28,4},{1,25},{... | collective-permute-start | bytes 786440 | tf_op jit(solution)/shard_map/ppermute | solution.py:39
  30.2 5.0 %collective-permute-done.9.refs_10_ = bf16[8,128,128]{2,1,0:T(8,128)(2,1)S(1)} collective-permute-done((bf16[8,128,128]{2,1,0:T(8,128)(2,1)S(1)}, bf16[8,128,128]{2,1,0:T(8,128)(2,1)S(1)}, u32[]{:S(2)}, u32[]{:S(2)}) %collective-permute-start.9) | collective-permute-done | bytes 262176 | tf_op jit(solution)/shard_map/ppermute | solution.py:39
  35.2 0.7 collective-permute-done.12.refs_1_
  35.9 0.0 collective-permute-start.6
  35.9 7.9 %collective-permute-done.13.refs_2_ = bf16[8,128,128]{2,1,0:T(8,128)(2,1)S(1)} collective-permute-done((bf16[8,128,128]{2,1,0:T(8,128)(2,1)S(1)}, bf16[8,128,128]{2,1,0:T(8,128)(2,1)S(1)}, u32[]{:S(2)}, u32[]{:S(2)}) %collective-permute-start.13) | collective-permute-done | bytes 262176 | tf_op jit(solution)/shard_map/ppermute | solution.py:39
  43.9 0.1 shard_map.90
  44.0 1.8 %collective-permute-start.15 = (bf16[2,128,128]{2,1,0:T(8,128)(2,1)S(1)}, bf16[2,128,128]{2,1,0:T(8,128)(2,1)S(1)}, u32[]{:S(2)}, u32[]{:S(2)}) collective-permute-start(bf16[2,128,128]{2,1,0:T(8,128)(2,1)S(1)} %get-tuple-element.22), channel_id=1, source_target_pairs={{0,1},{1,0},{2,3},{3,2},{4,5},{5,4},{6,7},{7,6},{8,9},{9,8},{10,11... | collective-permute-start | bytes 196616 | tf_op jit(solution)/shard_map/ppermute | solution.py:39
  45.7 0.0 collective-permute-done.4.refs_5_
  45.7 2.6 %collective-permute-start.16 = (bf16[2,128,128]{2,1,0:T(8,128)(2,1)S(1)}, bf16[2,128,128]{2,1,0:T(8,128)(2,1)S(1)}, u32[]{:S(2)}, u32[]{:S(2)}) collective-permute-start(bf16[2,128,128]{2,1,0:T(8,128)(2,1)S(1)} %get-tuple-element.23), channel_id=1, source_target_pairs={{0,2},{1,3},{2,0},{3,1},{4,6},{5,7},{6,4},{7,5},{8,10},{9,11},{10,... | collective-permute-start | bytes 196616 | tf_op jit(solution)/shard_map/ppermute | solution.py:39
  48.3 0.1 collective-permute-start.17
  48.5 5.1 %shard_map.85 = bf16[256,4096]{1,0:T(8,128)(2,1)} custom-call(bf16[256,14336]{1,0:T(8,128)(2,1)S(1)} %copy-done, s32[2,128]{1,0:T(2,128)S(1)} %pad_add_fusion.refs_0_, s32[2,128]{1,0:T(2,128)S(1)} %collective-permute-done.1.refs_1_, s32[2,128]{1,0:T(2,128)S(1)} %collective-permute-done.2.refs_2_, s32[2,128]{1,0:T(2,128)S(1)} %collective-permute-done.3.refs_3_, ...), custom_call_target="tpu_custom_call" | custom-call | flops 17179869184 | bytes 2097152 | tf_op jit(solution)/shard_map/pallas_call | solution.py:25
  53.6 0.0 collective-permute-done.15.refs_0_
  53.6 0.8 %collective-permute-done.17.refs_2_ = bf16[2,128,128]{2,1,0:T(8,128)(2,1)S(1)} collective-permute-done((bf16[2,128,128]{2,1,0:T(8,128)(2,1)S(1)}, bf16[2,128,128]{2,1,0:T(8,128)(2,1)S(1)}, u32[]{:S(2)}, u32[]{:S(2)}) %collective-permute-start.17) | collective-permute-done | bytes 65568 | tf_op jit(solution)/shard_map/ppermute | solution.py:39
  54.4 0.6 shard_map.91
  55.1 2.9 %collective-permute-start.20 = (bf16[2,128,128]{2,1,0:T(8,128)(2,1)S(1)}, bf16[2,128,128]{2,1,0:T(8,128)(2,1)S(1)}, u32[]{:S(2)}, u32[]{:S(2)}) collective-permute-start(bf16[2,128,128]{2,1,0:T(8,128)(2,1)S(1)} %get-tuple-element.26.refs_5_), channel_id=1, source_target_pairs={{0,3},{1,2},{2,1},{3,0},{4,7},{5,6},{6,5},{7,4},{8,11},{9,10},{10,... | collective-permute-start | bytes 196616 | tf_op jit(solution)/shard_map/ppermute | solution.py:39
  58.0 0.0 collective-permute-start.19
  58.0 1.5 %collective-permute-start.18 = (bf16[2,128,128]{2,1,0:T(8,128)(2,1)S(1)}, bf16[2,128,128]{2,1,0:T(8,128)(2,1)S(1)}, u32[]{:S(2)}, u32[]{:S(2)}) collective-permute-start(bf16[2,128,128]{2,1,0:T(8,128)(2,1)S(1)} %get-tuple-element.26.refs_5_), channel_id=1, source_target_pairs={{0,1},{1,0},{2,3},{3,2},{4,5},{5,4},{6,7},{7,6},{8,9},{9,8},{10,11... | collective-permute-start | bytes 196616 | tf_op jit(solution)/shard_map/ppermute | solution.py:39
  59.4 5.2 %all-to-all-start = ((f32[32,1,128]{2,1,0:T(1,128)}), f32[32,1,128]{2,1,0:T(1,128)S(1)}, u32[]{:S(2)}, u32[]{:S(2)}) async-start(f32[32,1,128]{2,1,0:T(1,128)} %bitcast.2), calls=%async_computation | async-start | bytes 32768 | tf_op jit(solution)/shard_map/all_to_all | solution.py:302
  64.6 0.0 copy-start.5
  64.6 0.9 %copy-done.5 = bf16[8,128,128]{2,1,0:T(8,128)(2,1)S(1)} copy-done((bf16[8,128,128]{2,1,0:T(8,128)(2,1)S(1)}, bf16[8,128,128]{2,1,0:T(8,128)(2,1)}, u32[]{:S(2)}) %copy-start.5) | copy-done | bytes 262168
  65.6 0.9 %copy-done.7 = bf16[8,128,128]{2,1,0:T(8,128)(2,1)S(1)} copy-done((bf16[8,128,128]{2,1,0:T(8,128)(2,1)S(1)}, bf16[8,128,128]{2,1,0:T(8,128)(2,1)}, u32[]{:S(2)}) %copy-start.7) | copy-done | bytes 262168
  66.5 0.9 %copy-done.9 = bf16[8,128,128]{2,1,0:T(8,128)(2,1)S(1)} copy-done((bf16[8,128,128]{2,1,0:T(8,128)(2,1)S(1)}, bf16[8,128,128]{2,1,0:T(8,128)(2,1)}, u32[]{:S(2)}) %copy-start.9) | copy-done | bytes 262168
  67.5 0.9 %copy-done.11 = bf16[8,128,128]{2,1,0:T(8,128)(2,1)S(1)} copy-done((bf16[8,128,128]{2,1,0:T(8,128)(2,1)S(1)}, bf16[8,128,128]{2,1,0:T(8,128)(2,1)}, u32[]{:S(2)}) %copy-start.11) | copy-done | bytes 262168
  68.4 7.2 %shard_map.86 = bf16[256,14336]{1,0:T(8,128)(2,1)} custom-call(bf16[256,4096]{1,0:T(8,128)(2,1)S(1)} %copy-done.2, s32[2,128]{1,0:T(2,128)S(1)} %pad_add_fusion.refs_0_, s32[2,128]{1,0:T(2,128)S(1)} %collective-permute-done.1.refs_1_, s32[2,128]{1,0:T(2,128)S(1)} %collective-permute-done.2.refs_2_, s32[2,128]{1,0:T(2,128)S(1)} %collective-permute-done.3.refs_3_, ...), custom_call_target="tpu_custom_call" | custom-call | flops 17179869184 | bytes 7340032 | tf_op jit(solution)/shard_map/pallas_call | solution.py:25
  75.6 0.0 all-to-all-done
  75.7 1.6 %shard_map.92 = f32[4,2,128,128]{3,2,1,0:T(8,128)} custom-call(s32[2,128]{1,0:T(2,128)S(1)} %pad_add_fusion.refs_0_, s32[2,128]{1,0:T(2,128)S(1)} %collective-permute-done.1.refs_1_, s32[2,128]{1,0:T(2,128)S(1)} %collective-permute-done.2.refs_2_, s32[2,128]{1,0:T(2,128)S(1)} %collective-permute-done.3.refs_3_, f32[32,128]{1,0:T(8,128)S(1)} %bitcast.7, ...), custom_call_target="tpu_custom_call" | custom-call | flops 67108864 | bytes 1048576 | tf_op jit(solution)/shard_map/pallas_call | solution.py:25
  (31 shorter events, 0.1 us)
Async XLA Ops:
  2.0 1.3 %collective-permute-start = (s32[1,128]{1,0:T(1,128)S(1)}, s32[1,128]{1,0:T(1,128)S(1)}, u32[]{:S(2)}, u32[]{:S(2)}) collective-permute-start(s32[1,128]{1,0:T(1,128)S(1)} %add_bitcast_fusion), channel_id=1, source_target_pairs={{0,4},{4,0},{8,12},{12,8},{16,20},{20,16},{24,28},{28,24},{1,5},{5... | collective-permute-start | bytes 1544 | tf_op jit(solution)/shard_map/ppermute | solution.py:39
  3.4 6.8 %collective-permute-start.3 = (s32[2,128]{1,0:T(2,128)S(1)}, s32[2,128]{1,0:T(2,128)S(1)}, u32[]{:S(2)}, u32[]{:S(2)}) collective-permute-start(s32[2,128]{1,0:T(2,128)S(1)} %pad_add_fusion.refs_0_), channel_id=1, source_target_pairs={{0,24},{4,28},{8,16},{12,20},{16,8},{20,12},{24,0},{28,4},{1,25},{... | collective-permute-start | bytes 3080 | tf_op jit(solution)/shard_map/ppermute | solution.py:39
  7.1 3.6 %collective-permute-start.2 = (s32[2,128]{1,0:T(2,128)S(1)}, s32[2,128]{1,0:T(2,128)S(1)}, u32[]{:S(2)}, u32[]{:S(2)}) collective-permute-start(s32[2,128]{1,0:T(2,128)S(1)} %pad_add_fusion.refs_0_), channel_id=1, source_target_pairs={{0,16},{4,20},{8,24},{12,28},{16,0},{20,4},{24,8},{28,12},{1,17},{... | collective-permute-start | bytes 3080 | tf_op jit(solution)/shard_map/ppermute | solution.py:39
  7.6 3.6 %collective-permute-start.1 = (s32[2,128]{1,0:T(2,128)S(1)}, s32[2,128]{1,0:T(2,128)S(1)}, u32[]{:S(2)}, u32[]{:S(2)}) collective-permute-start(s32[2,128]{1,0:T(2,128)S(1)} %pad_add_fusion.refs_0_), channel_id=1, source_target_pairs={{0,8},{4,12},{8,0},{12,4},{16,24},{20,28},{24,16},{28,20},{1,9},{5... | collective-permute-start | bytes 3080 | tf_op jit(solution)/shard_map/ppermute | solution.py:39
  7.8 1.6 %copy-start.1 = (bf16[256,4096]{1,0:T(8,128)(2,1)S(1)}, bf16[256,4096]{1,0:T(8,128)(2,1)}, u32[]{:S(2)}) copy-start(bf16[256,4096]{1,0:T(8,128)(2,1)} %cotangent.1) | copy-start | bytes 6291460
  9.4 3.1 %copy-start = (bf16[256,14336]{1,0:T(8,128)(2,1)S(1)}, bf16[256,14336]{1,0:T(8,128)(2,1)}, u32[]{:S(2)}) copy-start(bf16[256,14336]{1,0:T(8,128)(2,1)} %hidden.1) | copy-start | bytes 22020100
  10.1 5.7 %copy-start.3 = (bf16[8,128,128]{2,1,0:T(8,128)(2,1)S(1)}, bf16[8,128,128]{2,1,0:T(8,128)(2,1)}, u32[]{:S(2)}) copy-start(bf16[8,128,128]{2,1,0:T(8,128)(2,1)} %refs_4_.3) | copy-start | bytes 786436
  15.8 10.7 %collective-permute-start.11 = (bf16[4,8,128,128]{3,2,1,0:T(8,128)(2,1)S(1)}, bf16[4,8,128,128]{3,2,1,0:T(8,128)(2,1)S(1)}, u32[]{:S(2)}, u32[]{:S(2)}) collective-permute-start(bf16[4,8,128,128]{3,2,1,0:T(8,128)(2,1)S(1)} %get-tuple-element.16), channel_id=1, source_target_pairs={{0,4},{4,0},{8,12},{12,8},{16,20},{20,16},{24,28},{28,24},{1,5},{5... | collective-permute-start | bytes 3145736 | tf_op jit(solution)/shard_map/ppermute | solution.py:39
  15.9 8.8 %collective-permute-start.5 = (bf16[8,128,128]{2,1,0:T(8,128)(2,1)S(1)}, bf16[8,128,128]{2,1,0:T(8,128)(2,1)S(1)}, u32[]{:S(2)}, u32[]{:S(2)}) collective-permute-start(bf16[8,128,128]{2,1,0:T(8,128)(2,1)S(1)} %copy-done.3), channel_id=1, source_target_pairs={{0,8},{4,12},{8,0},{12,4},{16,24},{20,28},{24,16},{28,20},{1,9},{5... | collective-permute-start | bytes 786440 | tf_op jit(solution)/shard_map/ppermute | solution.py:39
  17.8 12.4 %collective-permute-start.7 = (bf16[8,128,128]{2,1,0:T(8,128)(2,1)S(1)}, bf16[8,128,128]{2,1,0:T(8,128)(2,1)S(1)}, u32[]{:S(2)}, u32[]{:S(2)}) collective-permute-start(bf16[8,128,128]{2,1,0:T(8,128)(2,1)S(1)} %copy-done.3), channel_id=1, source_target_pairs={{0,16},{4,20},{8,24},{12,28},{16,0},{20,4},{24,8},{28,12},{1,17},{... | collective-permute-start | bytes 786440 | tf_op jit(solution)/shard_map/ppermute | solution.py:39
  24.7 10.5 %collective-permute-start.9 = (bf16[8,128,128]{2,1,0:T(8,128)(2,1)S(1)}, bf16[8,128,128]{2,1,0:T(8,128)(2,1)S(1)}, u32[]{:S(2)}, u32[]{:S(2)}) collective-permute-start(bf16[8,128,128]{2,1,0:T(8,128)(2,1)S(1)} %collective-permute-done.5.refs_6_), channel_id=1, source_target_pairs={{0,16},{4,20},{8,24},{12,28},{16,0},{20,4},{24,8},{28,12},{1,17},{... | collective-permute-start | bytes 786440 | tf_op jit(solution)/shard_map/ppermute | solution.py:39
  26.7 9.2 %collective-permute-start.12 = (bf16[8,128,128]{2,1,0:T(8,128)(2,1)S(1)}, bf16[8,128,128]{2,1,0:T(8,128)(2,1)S(1)}, u32[]{:S(2)}, u32[]{:S(2)}) collective-permute-start(bf16[8,128,128]{2,1,0:T(8,128)(2,1)S(1)} %get-tuple-element.18), channel_id=1, source_target_pairs={{0,8},{4,12},{8,0},{12,4},{16,24},{20,28},{24,16},{28,20},{1,9},{5... | collective-permute-start | bytes 786440 | tf_op jit(solution)/shard_map/ppermute | solution.py:39
  28.2 15.6 %collective-permute-start.13 = (bf16[8,128,128]{2,1,0:T(8,128)(2,1)S(1)}, bf16[8,128,128]{2,1,0:T(8,128)(2,1)S(1)}, u32[]{:S(2)}, u32[]{:S(2)}) collective-permute-start(bf16[8,128,128]{2,1,0:T(8,128)(2,1)S(1)} %get-tuple-element.19), channel_id=1, source_target_pairs={{0,16},{4,20},{8,24},{12,28},{16,0},{20,4},{24,8},{28,12},{1,17},{... | collective-permute-start | bytes 786440 | tf_op jit(solution)/shard_map/ppermute | solution.py:39
  28.7 15.1 %collective-permute-start.14 = (bf16[8,128,128]{2,1,0:T(8,128)(2,1)S(1)}, bf16[8,128,128]{2,1,0:T(8,128)(2,1)S(1)}, u32[]{:S(2)}, u32[]{:S(2)}) collective-permute-start(bf16[8,128,128]{2,1,0:T(8,128)(2,1)S(1)} %get-tuple-element.20), channel_id=1, source_target_pairs={{0,24},{4,28},{8,16},{12,20},{16,8},{20,12},{24,0},{28,4},{1,25},{... | collective-permute-start | bytes 786440 | tf_op jit(solution)/shard_map/ppermute | solution.py:39
  30.2 15.5 %collective-permute-start.4 = (bf16[8,128,128]{2,1,0:T(8,128)(2,1)S(1)}, bf16[8,128,128]{2,1,0:T(8,128)(2,1)S(1)}, u32[]{:S(2)}, u32[]{:S(2)}) collective-permute-start(bf16[8,128,128]{2,1,0:T(8,128)(2,1)S(1)} %copy-done.3), channel_id=1, source_target_pairs={{0,4},{4,0},{8,12},{12,8},{16,20},{20,16},{24,28},{28,24},{1,5},{5... | collective-permute-start | bytes 786440 | tf_op jit(solution)/shard_map/ppermute | solution.py:39
  35.2 13.1 %collective-permute-start.8 = (bf16[8,128,128]{2,1,0:T(8,128)(2,1)S(1)}, bf16[8,128,128]{2,1,0:T(8,128)(2,1)S(1)}, u32[]{:S(2)}, u32[]{:S(2)}) collective-permute-start(bf16[8,128,128]{2,1,0:T(8,128)(2,1)S(1)} %collective-permute-done.7.refs_8_), channel_id=1, source_target_pairs={{0,4},{4,0},{8,12},{12,8},{16,20},{20,16},{24,28},{28,24},{1,5},{5... | collective-permute-start | bytes 786440 | tf_op jit(solution)/shard_map/ppermute | solution.py:39
  35.9 12.6 %collective-permute-start.6 = (bf16[8,128,128]{2,1,0:T(8,128)(2,1)S(1)}, bf16[8,128,128]{2,1,0:T(8,128)(2,1)S(1)}, u32[]{:S(2)}, u32[]{:S(2)}) collective-permute-start(bf16[8,128,128]{2,1,0:T(8,128)(2,1)S(1)} %collective-permute-done.5.refs_6_), channel_id=1, source_target_pairs={{0,4},{4,0},{8,12},{12,8},{16,20},{20,16},{24,28},{28,24},{1,5},{5... | collective-permute-start | bytes 786440 | tf_op jit(solution)/shard_map/ppermute | solution.py:39
  43.9 4.6 %collective-permute-start.10 = (bf16[8,128,128]{2,1,0:T(8,128)(2,1)S(1)}, bf16[8,128,128]{2,1,0:T(8,128)(2,1)S(1)}, u32[]{:S(2)}, u32[]{:S(2)}) collective-permute-start(bf16[8,128,128]{2,1,0:T(8,128)(2,1)S(1)} %collective-permute-done.9.refs_10_), channel_id=1, source_target_pairs={{0,4},{4,0},{8,12},{12,8},{16,20},{20,16},{24,28},{28,24},{1,5},{5... | collective-permute-start | bytes 786440 | tf_op jit(solution)/shard_map/ppermute | solution.py:39
  44.0 9.6 %collective-permute-start.15 = (bf16[2,128,128]{2,1,0:T(8,128)(2,1)S(1)}, bf16[2,128,128]{2,1,0:T(8,128)(2,1)S(1)}, u32[]{:S(2)}, u32[]{:S(2)}) collective-permute-start(bf16[2,128,128]{2,1,0:T(8,128)(2,1)S(1)} %get-tuple-element.22), channel_id=1, source_target_pairs={{0,1},{1,0},{2,3},{3,2},{4,5},{5,4},{6,7},{7,6},{8,9},{9,8},{10,11... | collective-permute-start | bytes 196616 | tf_op jit(solution)/shard_map/ppermute | solution.py:39
  45.7 7.8 %copy-start.4 = (bf16[8,128,128]{2,1,0:T(8,128)(2,1)}, bf16[8,128,128]{2,1,0:T(8,128)(2,1)S(1)}, u32[]{:S(2)}) copy-start(bf16[8,128,128]{2,1,0:T(8,128)(2,1)S(1)} %collective-permute-done.4.refs_5_) | copy-start | bytes 786436
  45.7 7.9 %collective-permute-start.16 = (bf16[2,128,128]{2,1,0:T(8,128)(2,1)S(1)}, bf16[2,128,128]{2,1,0:T(8,128)(2,1)S(1)}, u32[]{:S(2)}, u32[]{:S(2)}) collective-permute-start(bf16[2,128,128]{2,1,0:T(8,128)(2,1)S(1)} %get-tuple-element.23), channel_id=1, source_target_pairs={{0,2},{1,3},{2,0},{3,1},{4,6},{5,7},{6,4},{7,5},{8,10},{9,11},{10,... | collective-permute-start | bytes 196616 | tf_op jit(solution)/shard_map/ppermute | solution.py:39
  48.3 5.2 %copy-start.6 = (bf16[8,128,128]{2,1,0:T(8,128)(2,1)}, bf16[8,128,128]{2,1,0:T(8,128)(2,1)S(1)}, u32[]{:S(2)}) copy-start(bf16[8,128,128]{2,1,0:T(8,128)(2,1)S(1)} %collective-permute-done.8.refs_9_) | copy-start | bytes 786436
  48.3 16.3 %copy-start.2 = (bf16[256,4096]{1,0:T(8,128)(2,1)S(1)}, bf16[256,4096]{1,0:T(8,128)(2,1)}, u32[]{:S(2)}) copy-start(bf16[256,4096]{1,0:T(8,128)(2,1)} %cotangent.1) | copy-start | bytes 6291460
  48.3 6.1 %collective-permute-start.17 = (bf16[2,128,128]{2,1,0:T(8,128)(2,1)S(1)}, bf16[2,128,128]{2,1,0:T(8,128)(2,1)S(1)}, u32[]{:S(2)}, u32[]{:S(2)}) collective-permute-start(bf16[2,128,128]{2,1,0:T(8,128)(2,1)S(1)} %get-tuple-element.24), channel_id=1, source_target_pairs={{0,3},{1,2},{2,1},{3,0},{4,7},{5,6},{6,5},{7,4},{8,11},{9,10},{10,... | collective-permute-start | bytes 196616 | tf_op jit(solution)/shard_map/ppermute | solution.py:39
  48.5 5.1 %copy-start.8 = (bf16[8,128,128]{2,1,0:T(8,128)(2,1)}, bf16[8,128,128]{2,1,0:T(8,128)(2,1)S(1)}, u32[]{:S(2)}) copy-start(bf16[8,128,128]{2,1,0:T(8,128)(2,1)S(1)} %collective-permute-done.6.refs_7_) | copy-start | bytes 786436
  48.5 5.1 %copy-start.10 = (bf16[8,128,128]{2,1,0:T(8,128)(2,1)}, bf16[8,128,128]{2,1,0:T(8,128)(2,1)S(1)}, u32[]{:S(2)}) copy-start(bf16[8,128,128]{2,1,0:T(8,128)(2,1)S(1)} %collective-permute-done.10.refs_11_) | copy-start | bytes 786436
  55.1 20.6 %collective-permute-start.20 = (bf16[2,128,128]{2,1,0:T(8,128)(2,1)S(1)}, bf16[2,128,128]{2,1,0:T(8,128)(2,1)S(1)}, u32[]{:S(2)}, u32[]{:S(2)}) collective-permute-start(bf16[2,128,128]{2,1,0:T(8,128)(2,1)S(1)} %get-tuple-element.26.refs_5_), channel_id=1, source_target_pairs={{0,3},{1,2},{2,1},{3,0},{4,7},{5,6},{6,5},{7,4},{8,11},{9,10},{10,... | collective-permute-start | bytes 196616 | tf_op jit(solution)/shard_map/ppermute | solution.py:39
  58.0 17.7 %collective-permute-start.19 = (bf16[2,128,128]{2,1,0:T(8,128)(2,1)S(1)}, bf16[2,128,128]{2,1,0:T(8,128)(2,1)S(1)}, u32[]{:S(2)}, u32[]{:S(2)}) collective-permute-start(bf16[2,128,128]{2,1,0:T(8,128)(2,1)S(1)} %get-tuple-element.26.refs_5_), channel_id=1, source_target_pairs={{0,2},{1,3},{2,0},{3,1},{4,6},{5,7},{6,4},{7,5},{8,10},{9,11},{10,... | collective-permute-start | bytes 196616 | tf_op jit(solution)/shard_map/ppermute | solution.py:39
  58.0 17.7 %collective-permute-start.18 = (bf16[2,128,128]{2,1,0:T(8,128)(2,1)S(1)}, bf16[2,128,128]{2,1,0:T(8,128)(2,1)S(1)}, u32[]{:S(2)}, u32[]{:S(2)}) collective-permute-start(bf16[2,128,128]{2,1,0:T(8,128)(2,1)S(1)} %get-tuple-element.26.refs_5_), channel_id=1, source_target_pairs={{0,1},{1,0},{2,3},{3,2},{4,5},{5,4},{6,7},{7,6},{8,9},{9,8},{10,11... | collective-permute-start | bytes 196616 | tf_op jit(solution)/shard_map/ppermute | solution.py:39
  59.4 16.2 %all-to-all-start = ((f32[32,1,128]{2,1,0:T(1,128)}), f32[32,1,128]{2,1,0:T(1,128)S(1)}, u32[]{:S(2)}, u32[]{:S(2)}) async-start(f32[32,1,128]{2,1,0:T(1,128)} %bitcast.2), calls=%async_computation | async-start | bytes 32768 | tf_op jit(solution)/shard_map/all_to_all | solution.py:302
  64.6 1.0 %copy-start.5 = (bf16[8,128,128]{2,1,0:T(8,128)(2,1)S(1)}, bf16[8,128,128]{2,1,0:T(8,128)(2,1)}, u32[]{:S(2)}) copy-start(bf16[8,128,128]{2,1,0:T(8,128)(2,1)} %copy-done.4) | copy-start | bytes 786436
  65.6 0.9 %copy-start.7 = (bf16[8,128,128]{2,1,0:T(8,128)(2,1)S(1)}, bf16[8,128,128]{2,1,0:T(8,128)(2,1)}, u32[]{:S(2)}) copy-start(bf16[8,128,128]{2,1,0:T(8,128)(2,1)} %copy-done.6) | copy-start | bytes 786436
  66.5 0.9 %copy-start.9 = (bf16[8,128,128]{2,1,0:T(8,128)(2,1)S(1)}, bf16[8,128,128]{2,1,0:T(8,128)(2,1)}, u32[]{:S(2)}) copy-start(bf16[8,128,128]{2,1,0:T(8,128)(2,1)} %copy-done.8) | copy-start | bytes 786436
  67.5 0.9 %copy-start.11 = (bf16[8,128,128]{2,1,0:T(8,128)(2,1)S(1)}, bf16[8,128,128]{2,1,0:T(8,128)(2,1)}, u32[]{:S(2)}) copy-start(bf16[8,128,128]{2,1,0:T(8,128)(2,1)} %copy-done.10) | copy-start | bytes 786436

commit v2 on v1

v2 whole, which is shorter than its diff:
```python
import functools
import math

import jax
import jax.numpy as jnp
from jax import lax
from jax.experimental import pallas as pl
from jax.experimental.pallas import tpu as pltpu
from jax.sharding import PartitionSpec as P


F32, BF16 = jnp.float32, jnp.bfloat16
VMEM = pl.BlockSpec(memory_space=pltpu.VMEM)
SMEM = pl.BlockSpec(memory_space=pltpu.SMEM)
HBM = pl.BlockSpec(memory_space=pltpu.HBM)
UNROLL = 8
CHUNKS = 1


def shaped(dims, dtype):
    return jax.ShapeDtypeStruct(tuple(dims), dtype)


def kernel_call(body, out_shape, in_specs, out_specs, args, scratch=(), grid=(), limit=8, flops=0, moved=1 << 20):
    return pl.pallas_call(
        body,
        out_shape=out_shape,
        grid=grid,
        in_specs=in_specs,
        out_specs=out_specs,
        scratch_shapes=scratch,
        compiler_params=pltpu.CompilerParams(vmem_limit_bytes=limit << 20),
        cost_estimate=pl.CostEstimate(flops=flops, bytes_accessed=moved, transcendentals=0),
    )(*args)


def swap(value, axis, mask):
    size = lax.axis_size(axis)
    return lax.ppermute(value, axis, [(i, i ^ mask) for i in range(size)])


def turned(m, pairs):
    bits = pairs.bit_length() - 1
    half = bits // 2
    return (m >> half) | ((m & ((1 << half) - 1)) << (bits - half))


def chip_swap(value, m):
    size = lax.axis_size("fsdp")
    masks = (2 * m, 2 * turned(m, size // 2))
    return lax.ppermute(value, "fsdp", [(i, i ^ masks[i & 1]) for i in range(size)])


def lanes(block, edge):
    return pl.ds(pl.multiple_of(block * edge, edge), edge)


def contract(left, right, left_dim, right_dim):
    dims = (((left_dim,), (right_dim,)), ((), ()))
    return lax.dot_general(left, right, dims, preferred_element_type=F32)


def pair_kernel(own, other, out):
    out[0:1] = own[...]
    out[1:2] = other[...]


def stage_kernel(edge, cotangent, flipped):
    def step(i, carry):
        for u in range(UNROLL):
            block = i * UNROLL + u
            flipped[block] = cotangent[:, lanes(block, edge)].T
        return carry

    lax.fori_loop(0, flipped.shape[0] // UNROLL, step, 0)


def terms_kernel(slots, edge, span, flipped, hidden, *refs):
    mine, theirs, where, rows, cols = refs[-5:]
    metas = refs[:-5]
    pairs, width = mine.shape[0], mine.shape[1]
    for parity, target in ((0, mine), (1, theirs)):
        target[...] = jnp.zeros(target.shape, target.dtype)

        end = jnp.int32(0)
        for pair in range(pairs):
            meta = metas[turned(pair, pairs) if parity else pair]
            for j in span:
                where[end] = pair * width + (j - span[0])
                rows[end] = meta[parity, j]
                cols[end] = meta[parity, slots + j]
                end = end + (j < meta[parity, 2 * slots]).astype(jnp.int32)
        last = jnp.maximum(end - 1, 0)
        for u in range(UNROLL - 1):
            where[end + u] = where[last]
            rows[end + u] = rows[last]
            cols[end + u] = cols[last]

        def step(i, carry):
            for u in range(UNROLL):
                at = i * UNROLL + u
                term = contract(flipped[cols[at]], hidden[:, lanes(rows[at], edge)], 1, 0)
                spot = where[at]
                target[spot // width, spot % width] = term.astype(target.dtype)
            return carry

        lax.fori_loop(0, (end + UNROLL - 1) // UNROLL, step, 0)


def fold_kernel(mine, arrived, own, sent):
    half = own.shape[0]
    own[...] = mine[:half] + arrived[:half].astype(F32)
    sent[...] = (mine[half:] + arrived[half:].astype(F32)).astype(BF16)


def in_plane_kernel(share, mine, arrived, *outs):
    place = lax.axis_index("dp")
    for m, out in enumerate(outs):
        at = pl.ds((place ^ m) * share, share)
        out[...] = (mine[0, at] + arrived[0, at].astype(F32)).astype(out.dtype)


def settle_kernel(own, *refs):
    arrived, final, squares = refs[:-2], refs[-2], refs[-1]
    total = pair_sum([own[...]] + [ref[...].astype(F32) for ref in arrived])
    squared = jnp.sum(jnp.sum(total * total, axis=0), axis=0, keepdims=True)
    squares[...] = jnp.broadcast_to(squared[:, None, :], squares.shape)
    for i in range(total.shape[0]):
        final[i] = total[i].T.astype(BF16)


def finish_kernel(root_tokens, slots, edge, chunks, pairs, *refs):
    metas, squares, pieces, out = refs[:pairs], refs[pairs : pairs + chunks], refs[pairs + chunks : -1], refs[-1]
    place = lax.axis_index("dp")
    live = 0
    for meta in metas:
        live = live + meta[0, 2 * slots] + meta[1, 2 * slots]
    entries = live.astype(F32) * (edge * edge)
    total = pair_sum([jnp.sum(ref[:, 0, :], keepdims=True) for ref in squares])
    spread = jnp.sqrt(total / entries)
    factor = jnp.minimum(1.0, 0.5 * root_tokens / spread) / root_tokens
    per_chunk = len(pieces) // chunks
    for i, piece in enumerate(pieces):
        chunk, m = i // per_chunk, i % per_chunk
        out[chunk * per_chunk + (place ^ m)] = piece[...].astype(F32) * factor[:, :, None]


def lists_kernel(slots, plans, *refs):
    metas, lists = refs[:-1], refs[-1]
    pairs = len(metas)
    for plan, (out_at, in_at, blocks, steps) in enumerate(plans):
        picks, sources, nexts, heads, filled, starts = range(6 * plan, 6 * plan + 6)
        for block in range(blocks):
            lists[heads, block] = -1
        at = jnp.int32(0)
        for owner in range(2 * pairs):
            pair, side = owner // 2, owner % 2
            meta = metas[turned(pair, pairs) if side else pair]
            count = meta[side, 2 * slots]
            for j in range(slots):
                block = jnp.where(j < count, meta[side, out_at * slots + j], blocks)
                lists[picks, at] = owner * slots + j
                lists[sources, at] = meta[side, in_at * slots + j]
                lists[nexts, at] = lists[heads, block]
                lists[heads, block] = at
                at = at + (j < count).astype(jnp.int32)
        last = jnp.maximum(at - 1, 0)
        for u in range(UNROLL - 1):
            lists[picks, at + u] = lists[picks, last]
            lists[sources, at + u] = lists[sources, last]
        lists[starts, steps + 1] = at
        group = blocks // steps
        at = jnp.int32(0)
        for block in range(blocks):
            if block % group == 0:
                lists[starts, block // group] = at
            lists[filled, at] = block % group
            at = at + (lists[heads, block] >= 0).astype(jnp.int32)
        lists[starts, steps] = at


def products_kernel(edge, row, steps, flip, lists, source, *refs):
    made, refs = refs[-1], refs[:-1]
    if len(refs) > 2:
        weights, out, held = refs[:-2], refs[-2], refs[-1]
    else:
        weights, (held, out) = (), refs
    picks, sources, nexts, heads, filled, starts = range(row, row + 6)
    group = out.shape[1] // edge

    @pl.when(pl.program_id(0) == 0)
    def _():
        for owner, ref in enumerate(weights):
            count = ref.shape[0]
            held[owner * count : (owner + 1) * count] = ref[...]

        def step(i, carry):
            for u in range(UNROLL):
                spot = i * UNROLL + u
                left = source[:, lanes(lists[sources, spot], edge)]
                made[spot] = contract(left, held[lists[picks, spot]], 1, 1 if flip else 0)
            return carry

        lax.fori_loop(0, (lists[starts, steps + 1] + UNROLL - 1) // UNROLL, step, 0)

    turn = pl.program_id(0)
    out[...] = jnp.zeros(out.shape, out.dtype)

    def fill(i, carry):
        block = lists[filled, i]
        first = lists[heads, turn * group + block]

        def more(s):
            made[first] += made[s]
            return lists[nexts, s]

        lax.while_loop(lambda s: s >= 0, more, lists[nexts, first])
        out[:, lanes(block, edge)] = made[first].astype(out.dtype)
        return carry

    lax.fori_loop(lists[starts, turn], lists[starts, turn + 1], fill, 0)


def products(lists, row, source, weights, width, total, edge, flip, steps):
    tokens = source.shape[0]
    block = pl.BlockSpec((tokens, width // steps), lambda i: (0, i))
    shape, spec = shaped((tokens, width), BF16), block
    if len(weights) > 1:
        shape = (shape, shaped((total, edge, edge), BF16))
        spec = (spec, pl.BlockSpec((total, edge, edge), lambda i: (0, 0, 0)))
    return kernel_call(
        functools.partial(products_kernel, edge, row, steps, flip),
        shape,
        [SMEM] + [VMEM] * (1 + len(weights)),
        spec,
        [lists, source] + weights,
        scratch=[pltpu.VMEM((total + UNROLL, tokens, edge), F32)],
        grid=(steps,),
        limit=24 if total <= 64 else 63,
        flops=1 << 34,
        moved=tokens * width * 2,
    )


def pair_sum(terms):
    while len(terms) > 1:
        terms = [a + b for a, b in zip(terms[::2], terms[1::2])]
    return terms[0]


def shards(hidden, cotangent, tiles, tile_rows, tile_cols, counts):
    n_fsdp, n_dp = lax.axis_size("fsdp"), lax.axis_size("dp")
    tokens = hidden.shape[0]
    slots, edge = tiles.shape[0], tiles.shape[1]
    pairs = n_fsdp // 2
    width = slots // CHUNKS
    share = width // n_dp
    blocks_model = cotangent.shape[1] // edge
    root_tokens = math.sqrt(tokens * n_fsdp * n_dp)
    apart = range(1, pairs)

    filler = jnp.zeros((128 - 2 * slots - 1,), jnp.int32)
    packed = jnp.concatenate([tile_rows, tile_cols, counts, filler])[None]
    near = kernel_call(
        pair_kernel,
        shaped((2, packed.shape[1]), jnp.int32),
        [VMEM, VMEM],
        VMEM,
        [packed, swap(packed, "fsdp", 1)],
        flops=1 << 34,
    )
    metas = [near] + [chip_swap(near, m) for m in apart]

    across = [tiles]
    for m in apart:
        low = m & -m
        across.append(chip_swap(across[m ^ low], low))
    beside = [swap(across[m], "fsdp", 1) for m in range(pairs)]
    weights = [w for both in zip(across, beside) for w in both]

    flipped = kernel_call(
        functools.partial(stage_kernel, edge),
        shaped((blocks_model, edge, tokens), BF16),
        [VMEM],
        VMEM,
        [cotangent],
        flops=1 << 30,
        moved=4 << 20,
    )

    squares, pieces = [], []
    for c in range(CHUNKS):
        span = range(c * width, (c + 1) * width)
        dims = (pairs, width, edge, edge)
        mine, theirs = kernel_call(
            functools.partial(terms_kernel, slots, edge, span),
            (shaped(dims, F32), shaped(dims, BF16)),
            [VMEM, VMEM] + [SMEM] * pairs,
            (VMEM, VMEM),
            [flipped, hidden] + metas,
            scratch=[pltpu.SMEM((pairs * width + UNROLL,), jnp.int32)] * 3,
            limit=16,
            flops=4 * pairs * width * tokens * edge * edge,
        )
        arrived = swap(theirs, "fsdp", 1)
        own, step = mine, 0
        while own.shape[0] > 1:
            half = (own.shape[0] // 2,) + dims[1:]
            own, sent = kernel_call(
                fold_kernel,
                (shaped(half, F32), shaped(half, BF16)),
                [VMEM, VMEM],
                (VMEM, VMEM),
                [own, arrived],
                flops=1 << 33,
                limit=8 if pairs <= 4 else 40,
            )
            arrived = chip_swap(sent, half[0])
            step += 1
        piece = (share, edge, edge)
        own, *sent = kernel_call(
            functools.partial(in_plane_kernel, share),
            (shaped(piece, F32),) + (shaped(piece, BF16),) * (n_dp - 1),
            [VMEM] * 2,
            (VMEM,) * n_dp,
            [own, arrived],
            flops=1 << 33,
        )
        arrived = [swap(sent[m - 1], "dp", m) for m in range(1, n_dp)]
        final, squared = kernel_call(
            settle_kernel,
            (shaped(piece, BF16), shaped((n_fsdp * n_dp, 1, edge), F32)),
            [VMEM] * n_dp,
            (VMEM, VMEM),
            [own] + arrived,
            flops=1 << 33,
        )
        pieces += [final] + [swap(final, "dp", m) for m in range(1, n_dp)]
        squares.append(lax.all_to_all(squared, ("fsdp", "dp"), 0, 0, tiled=True))

    blocks_ff, total = hidden.shape[1] // edge, n_fsdp * slots
    plans = ((1, 0, blocks_model, 2), (0, 1, blocks_ff, 4))
    room = -(-max(total + UNROLL, blocks_ff + 1, blocks_model + 1) // 128) * 128
    lists = kernel_call(
        functools.partial(lists_kernel, slots, plans),
        shaped((6 * len(plans), room), jnp.int32),
        [SMEM] * pairs,
        SMEM,
        metas,
        flops=1 << 30,
    )
    layer_out, held = products(
        lists, 0, hidden, weights, cotangent.shape[1], total, edge, False, plans[0][3]
    )
    hidden_grad = products(
        lists, 6, cotangent, [held], hidden.shape[1], total, edge, True, plans[1][3]
    )
    weight_grad = kernel_call(
        functools.partial(finish_kernel, root_tokens, slots, edge, CHUNKS, pairs),
        shaped((CHUNKS * n_dp, share, edge, edge), F32),
        [SMEM] * pairs + [VMEM] * (len(squares) + len(pieces)),
        VMEM,
        metas + squares + pieces,
        flops=1 << 33,
    )
    return layer_out, hidden_grad, weight_grad.reshape(slots, edge, edge)


def solution(mesh):
    placed = (
        P(("fsdp", "dp"), None),
        P(("fsdp", "dp"), None),
        P("fsdp", None, None),
        P("fsdp"),
        P("fsdp"),
        P("fsdp"),
    )
    return jax.shard_map(
        shards,
        mesh=mesh,
        in_specs=placed,
        out_specs=(P(("fsdp", "dp"), None), P(("fsdp", "dp"), None), P("fsdp", None, None)),
        check_vma=False,
    )
```

time: 77.6 us -> 72 us (0.928)
  local copies, waits for them, and re-layouts: 6.64 us -> 1.61 us
  starting transfers between devices: 27.8 us -> 24.5 us
  Pallas kernels: 18.9 us -> 22 us
    ppermute x21 -> x12, waiting for transfers between devices: 21.7 us -> 4.33 us  [swap(): return lax.ppermute(value, axis, [(i, i ^ mask) for i in range(size)])]
    ppermute x0 -> x8, waiting for transfers between devices: none -> 17.1 us  [chip_swap(): lax.ppermute(value, 'fsdp', [(i, i ^ masks[i & 1]) for i in range(size)])]
    ppermute x21 -> x12, starting transfers between devices: 22.7 us -> 10.5 us  [swap(): return lax.ppermute(value, axis, [(i, i ^ mask) for i in range(size)])]
    ppermute x0 -> x8, starting transfers between devices: none -> 9.24 us  [chip_swap(): lax.ppermute(value, 'fsdp', [(i, i ^ masks[i & 1]) for i in range(size)])]
    unnamed x24 -> x12, local copies, waits for them, and re-layouts: 6.64 us -> 1.61 us
    pallas_call x8 -> x11, Pallas kernels: 18.9 us -> 22 us  [kernel_call(): pl.pallas_call(body, out_shape=out_shape, grid=grid, in_specs=in_specs, o...]
  transfers between devices with their start and end apart: 22 -> 21, of which waited for: 8 -> 8; matrix products, arithmetic and copies ran while one was open for 0% -> 0% of each run, Pallas kernels for 17% -> 23%
where the time goes in v2:
time: 72 us; the launch traced here: 71.8 us
  starting transfers between devices  24.5 us (34%)
  Pallas kernels  22 us (31%)
  waiting for transfers between devices  21.4 us (30%)
  local copies, waits for them, and re-layouts  1.61 us (2%)
  between operations  1.39 us (2%)
  other arithmetic  0.9 us (1%)
    pallas_call x11, Pallas kernels, kernel_call(): pl.pallas_call(body, out_shape=out_shape, grid=grid, in_specs=in_specs, o...  22 us
    ppermute x8, waiting for transfers between devices, chip_swap(): lax.ppermute(value, 'fsdp', [(i, i ^ masks[i & 1]) for i in range(size)])  17.1 us
    ppermute x12, starting transfers between devices, swap(): return lax.ppermute(value, axis, [(i, i ^ mask) for i in range(size)])  10.5 us
    ppermute x8, starting transfers between devices, chip_swap(): lax.ppermute(value, 'fsdp', [(i, i ^ masks[i & 1]) for i in range(size)])  9.24 us
    all_to_all x1, starting transfers between devices, shards(): squares.append(lax.all_to_all(squared, ('fsdp', 'dp'), 0, 0, tiled=True))  4.73 us
    ppermute x12, waiting for transfers between devices, swap(): return lax.ppermute(value, axis, [(i, i ^ mask) for i in range(size)])  4.33 us
    unnamed x12, local copies, waits for them, and re-layouts  1.61 us
  transfers between devices with their start and end apart: 21, of which 8 were waited for; matrix products, arithmetic and copies ran while one was open for 0% of the time, Pallas kernels for 23%

profile of v2, /device:TPU:0, one launch (start us, length us, event | category | flops | bytes accessed | tf_op | source)
XLA Modules:
  0.0 71.8 jit_solution(6249459419214853418)
XLA Ops:
  1.3 0.0 slice-start
  1.3 0.9 %add_bitcast_fusion.own = s32[1,128]{1,0:T(1,128)S(1)} fusion(s32[111]{0:T(128)S(1)} %broadcast_in_dim.6, s32[1]{0:T(128)S(6)} %copy.9, s32[8]{0:T(128)} %param.10, s32[8]{0:T(128)} %param.9), kind=kLoop, calls=%fused_computation | loop fusion | flops 384 | bytes 1024 | tf_op jit(solution)/shard_map/broadcast_in_dim | solution.py:263
  2.2 0.5 collective-permute-start
  2.7 0.8 %collective-permute-done.other = s32[1,128]{1,0:T(1,128)S(1)} collective-permute-done((s32[1,128]{1,0:T(1,128)S(1)}, s32[1,128]{1,0:T(1,128)S(1)}, u32[]{:S(2)}, u32[]{:S(2)}) %collective-permute-start) | collective-permute-done | bytes 544 | tf_op jit(solution)/shard_map/ppermute | solution.py:39
  3.6 3.8 %collective-permute-start.3 = (s32[2,128]{1,0:T(2,128)S(1)}, s32[2,128]{1,0:T(2,128)S(1)}, u32[]{:S(2)}, u32[]{:S(2)}) collective-permute-start(s32[2,128]{1,0:T(2,128)S(1)} %shard_map.85.refs_0_), channel_id=1, source_target_pairs={{0,24},{4,28},{8,16},{12,20},{16,8},{20,12},{24,0},{28,4},{1,25},{... | collective-permute-start | bytes 3080 | tf_op jit(solution)/shard_map/ppermute | solution.py:51
  7.3 0.5 collective-permute-start.2
  7.8 0.1 collective-permute-start.1
  7.9 0.8 %shard_map.89.flipped = bf16[32,128,256]{2,1,0:T(8,128)(2,1)S(1)} custom-call(bf16[256,4096]{1,0:T(8,128)(2,1)S(1)} %copy-done), custom_call_target="tpu_custom_call" | custom-call | flops 1073741824 | bytes 4194304 | tf_op jit(solution)/shard_map/pallas_call | solution.py:25
  8.7 0.2 collective-permute-done.3.refs_3_
  8.9 2.0 %collective-permute-done.2.refs_2_ = s32[2,128]{1,0:T(2,128)S(1)} collective-permute-done((s32[2,128]{1,0:T(2,128)S(1)}, s32[2,128]{1,0:T(2,128)S(1)}, u32[]{:S(2)}, u32[]{:S(2)}) %collective-permute-start.2) | collective-permute-done | bytes 1056 | tf_op jit(solution)/shard_map/ppermute | solution.py:51
  10.9 0.5 collective-permute-done.1.refs_1_
  11.4 3.3 %shard_map.90 = (f32[4,8,128,128]{3,2,1,0:T(8,128)S(1)}, bf16[4,8,128,128]{3,2,1,0:T(8,128)(2,1)S(1)}) custom-call(bf16[32,128,256]{2,1,0:T(8,128)(2,1)S(1)} %shard_map.89.flipped, bf16[256,14336]{1,0:T(8,128)(2,1)S(1)} %bitcast.4, s32[2,128]{1,0:T(2,128)S(1)} %shard_map.85.refs_0_, s32[2,128]{1,0:T(2,128)S(1)} %collective-permute-done.1.refs_1_, ...), custom_call_target="tpu_custom_call" | custom-call | flops 536870912 | bytes 1048576 | tf_op jit(solution)/shard_map/pallas_call | solution.py:25
  14.7 0.1 collective-permute-start.11
  14.8 2.6 %collective-permute-done.11.arrived = bf16[4,8,128,128]{3,2,1,0:T(8,128)(2,1)S(1)} collective-permute-done((bf16[4,8,128,128]{3,2,1,0:T(8,128)(2,1)S(1)}, bf16[4,8,128,128]{3,2,1,0:T(8,128)(2,1)S(1)}, u32[]{:S(2)}, u32[]{:S(2)}) %collective-permute-start.11) | collective-permute-done | bytes 1048608 | tf_op jit(solution)/shard_map/ppermute | solution.py:39
  17.5 0.2 shard_map.91
  17.6 1.6 %collective-permute-start.12 = (bf16[2,8,128,128]{3,2,1,0:T(8,128)(2,1)S(1)}, bf16[2,8,128,128]{3,2,1,0:T(8,128)(2,1)S(1)}, u32[]{:S(2)}, u32[]{:S(2)}) collective-permute-start(bf16[2,8,128,128]{3,2,1,0:T(8,128)(2,1)S(1)} %get-tuple-element.22), channel_id=1, source_target_pairs={{0,16},{4,12},{8,24},{12,4},{16,0},{20,28},{24,8},{28,20},{1,17},{... | collective-permute-start | bytes 1572872 | tf_op jit(solution)/shard_map/ppermute | solution.py:51
  19.2 0.7 collective-permute-start.7
  19.9 0.5 collective-permute-start.5
  20.5 12.0 %collective-permute-done.7.refs_4_ = bf16[8,128,128]{2,1,0:T(8,128)(2,1)S(1)} collective-permute-done((bf16[8,128,128]{2,1,0:T(8,128)(2,1)S(1)}, bf16[8,128,128]{2,1,0:T(8,128)(2,1)S(1)}, u32[]{:S(2)}, u32[]{:S(2)}) %collective-permute-start.7) | collective-permute-done | bytes 262176 | tf_op jit(solution)/shard_map/ppermute | solution.py:51
  32.5 0.1 collective-permute-start.9
  32.6 0.0 collective-permute-done.12.arrived
  32.6 0.1 shard_map.92
  32.7 2.0 %collective-permute-start.13 = (bf16[1,8,128,128]{3,2,1,0:T(8,128)(2,1)S(1)}, bf16[1,8,128,128]{3,2,1,0:T(8,128)(2,1)S(1)}, u32[]{:S(2)}, u32[]{:S(2)}) collective-permute-start(bf16[1,8,128,128]{3,2,1,0:T(8,128)(2,1)S(1)} %get-tuple-element.24), channel_id=1, source_target_pairs={{0,8},{4,20},{8,0},{12,28},{16,24},{20,4},{24,16},{28,12},{1,9},{5... | collective-permute-start | bytes 786440 | tf_op jit(solution)/shard_map/ppermute | solution.py:51
  34.7 3.6 %shard_map.86.lists = s32[12,128]{1,0:T(8,128)S(1)} custom-call(s32[2,128]{1,0:T(2,128)S(1)} %shard_map.85.refs_0_, s32[2,128]{1,0:T(2,128)S(1)} %collective-permute-done.1.refs_1_, s32[2,128]{1,0:T(2,128)S(1)} %collective-permute-done.2.refs_2_, s32[2,128]{1,0:T(2,128)S(1)} %collective-permute-done.3.refs_3_), custom_call_target="tpu_custom_call" | custom-call | flops 1073741824 | bytes 1048576 | tf_op jit(solution)/shard_map/pallas_call | solution.py:25
  38.3 0.6 collective-permute-start.8
  38.9 0.1 collective-permute-start.6
  39.0 0.0 collective-permute-done.9.refs_6_
  39.0 0.4 collective-permute-start.10
  39.4 2.3 %collective-permute-done.13.arrived = bf16[1,8,128,128]{3,2,1,0:T(8,128)(2,1)S(1)} collective-permute-done((bf16[1,8,128,128]{3,2,1,0:T(8,128)(2,1)S(1)}, bf16[1,8,128,128]{3,2,1,0:T(8,128)(2,1)S(1)}, u32[]{:S(2)}, u32[]{:S(2)}) %collective-permute-start.13) | collective-permute-done | bytes 262176 | tf_op jit(solution)/shard_map/ppermute | solution.py:51
  41.7 1.6 %collective-permute-start.14 = (bf16[2,128,128]{2,1,0:T(8,128)(2,1)S(1)}, bf16[2,128,128]{2,1,0:T(8,128)(2,1)S(1)}, u32[]{:S(2)}, u32[]{:S(2)}) collective-permute-start(bf16[2,128,128]{2,1,0:T(8,128)(2,1)S(1)} %get-tuple-element.26), channel_id=1, source_target_pairs={{0,1},{1,0},{2,3},{3,2},{4,5},{5,4},{6,7},{7,6},{8,9},{9,8},{10,11... | collective-permute-start | bytes 196616 | tf_op jit(solution)/shard_map/ppermute | solution.py:39
  43.4 0.0 collective-permute-done.4.refs_1_
  43.4 2.6 %collective-permute-start.15 = (bf16[2,128,128]{2,1,0:T(8,128)(2,1)S(1)}, bf16[2,128,128]{2,1,0:T(8,128)(2,1)S(1)}, u32[]{:S(2)}, u32[]{:S(2)}) collective-permute-start(bf16[2,128,128]{2,1,0:T(8,128)(2,1)S(1)} %get-tuple-element.27), channel_id=1, source_target_pairs={{0,2},{1,3},{2,0},{3,1},{4,6},{5,7},{6,4},{7,5},{8,10},{9,11},{10,... | collective-permute-start | bytes 196616 | tf_op jit(solution)/shard_map/ppermute | solution.py:39
  46.0 0.0 collective-permute-done.6.refs_3_
  46.0 0.2 collective-permute-start.16
  46.2 5.0 %shard_map.87 = (bf16[256,4096]{1,0:T(8,128)(2,1)}, bf16[64,128,128]{2,1,0:T(8,128)(2,1)S(1)}) custom-call(s32[12,128]{1,0:T(8,128)S(1)} %shard_map.86.lists, bf16[256,14336]{1,0:T(8,128)(2,1)S(1)} %bitcast.4, bf16[8,128,128]{2,1,0:T(8,128)(2,1)S(1)} %copy-done.1, bf16[8,128,128]{2,1,0:T(8,128)(2,1)S(1)} %collective-permute-done.4.refs_1_, ...), custom_call_target="tpu_custom_call" | custom-call | flops 17179869184 | bytes 2097152 | tf_op jit(solution)/shard_map/pallas_call | solution.py:25
  51.2 0.0 collective-permute-done.14.refs_0_
  51.2 0.0 collective-permute-done.15.refs_1_
  51.2 0.8 %collective-permute-done.16.refs_2_ = bf16[2,128,128]{2,1,0:T(8,128)(2,1)S(1)} collective-permute-done((bf16[2,128,128]{2,1,0:T(8,128)(2,1)S(1)}, bf16[2,128,128]{2,1,0:T(8,128)(2,1)S(1)}, u32[]{:S(2)}, u32[]{:S(2)}) %collective-permute-start.16) | collective-permute-done | bytes 65568 | tf_op jit(solution)/shard_map/ppermute | solution.py:39
  52.0 0.7 shard_map.94
  52.7 3.4 %collective-permute-start.19 = (bf16[2,128,128]{2,1,0:T(8,128)(2,1)S(1)}, bf16[2,128,128]{2,1,0:T(8,128)(2,1)S(1)}, u32[]{:S(2)}, u32[]{:S(2)}) collective-permute-start(bf16[2,128,128]{2,1,0:T(8,128)(2,1)S(1)} %get-tuple-element.30.refs_5_), channel_id=1, source_target_pairs={{0,3},{1,2},{2,1},{3,0},{4,7},{5,6},{6,5},{7,4},{8,11},{9,10},{10,... | collective-permute-start | bytes 196616 | tf_op jit(solution)/shard_map/ppermute | solution.py:39
  56.1 1.0 %collective-permute-start.17 = (bf16[2,128,128]{2,1,0:T(8,128)(2,1)S(1)}, bf16[2,128,128]{2,1,0:T(8,128)(2,1)S(1)}, u32[]{:S(2)}, u32[]{:S(2)}) collective-permute-start(bf16[2,128,128]{2,1,0:T(8,128)(2,1)S(1)} %get-tuple-element.30.refs_5_), channel_id=1, source_target_pairs={{0,1},{1,0},{2,3},{3,2},{4,5},{5,4},{6,7},{7,6},{8,9},{9,8},{10,11... | collective-permute-start | bytes 196616 | tf_op jit(solution)/shard_map/ppermute | solution.py:39
  57.1 4.7 %all-to-all-start = ((f32[32,1,128]{2,1,0:T(1,128)}), f32[32,1,128]{2,1,0:T(1,128)S(1)}, u32[]{:S(2)}, u32[]{:S(2)}) async-start(f32[32,1,128]{2,1,0:T(1,128)} %get-tuple-element.29), calls=%async_computation | async-start | bytes 32768 | tf_op jit(solution)/shard_map/all_to_all | solution.py:339
  61.8 0.0 copy-start.3
  61.9 1.6 %copy-done.3 = bf16[64,128,128]{2,1,0:T(8,128)(2,1)S(1)} copy-done((bf16[64,128,128]{2,1,0:T(8,128)(2,1)S(1)}, bf16[64,128,128]{2,1,0:T(8,128)(2,1)}, u32[]{:S(2)}) %copy-start.3) | copy-done | bytes 2097176
  63.4 6.8 %shard_map.88 = bf16[256,14336]{1,0:T(8,128)(2,1)} custom-call(s32[12,128]{1,0:T(8,128)S(1)} %shard_map.86.lists, bf16[256,4096]{1,0:T(8,128)(2,1)S(1)} %copy-done, bf16[64,128,128]{2,1,0:T(8,128)(2,1)S(1)} %copy-done.3), custom_call_target="tpu_custom_call" | custom-call | flops 17179869184 | bytes 7340032 | tf_op jit(solution)/shard_map/pallas_call | solution.py:25
  70.3 0.0 collective-permute-done.19.refs_8_
  70.3 0.0 collective-permute-done.18.refs_7_
  70.3 1.6 %shard_map.95 = f32[4,2,128,128]{3,2,1,0:T(8,128)} custom-call(s32[2,128]{1,0:T(2,128)S(1)} %shard_map.85.refs_0_, s32[2,128]{1,0:T(2,128)S(1)} %collective-permute-done.1.refs_1_, s32[2,128]{1,0:T(2,128)S(1)} %collective-permute-done.2.refs_2_, s32[2,128]{1,0:T(2,128)S(1)} %collective-permute-done.3.refs_3_, f32[32,1,128]{2,1,0:T(1,128)S(1)} %all-to-all-done.refs_4_, ...), custom_call_target="tpu_custom_call" | custom-call | flops 8589934592 | bytes 1048576 | tf_op jit(solution)/shard_map/pallas_call | solution.py:25
  (20 shorter events, 0.1 us)
Async XLA Ops:
  1.3 10.1 %slice-start = ((s8[7340032]{0:T(1024)(128)(4,1)}), s8[4194304]{0:T(1024)(128)(4,1)S(1)}, s32[]{:S(2)}) async-start(s8[7340032]{0:T(1024)(128)(4,1)} %bitcast.3), calls=%async_computation.1 | async-start | bytes 8388608
  2.2 5.7 %copy-start = (bf16[256,4096]{1,0:T(8,128)(2,1)S(1)}, bf16[256,4096]{1,0:T(8,128)(2,1)}, u32[]{:S(2)}) copy-start(bf16[256,4096]{1,0:T(8,128)(2,1)} %cotangent.1) | copy-start | bytes 6291460
  2.2 9.2 %slice-start.1 = ((s8[7340032]{0:T(1024)(128)(4,1)}), s8[3145728]{0:T(1024)(128)(4,1)S(1)}, s32[]{:S(2)}) async-start(s8[7340032]{0:T(1024)(128)(4,1)} %bitcast.3), calls=%async_computation.2 | async-start | bytes 6291456
  2.2 1.4 %collective-permute-start = (s32[1,128]{1,0:T(1,128)S(1)}, s32[1,128]{1,0:T(1,128)S(1)}, u32[]{:S(2)}, u32[]{:S(2)}) collective-permute-start(s32[1,128]{1,0:T(1,128)S(1)} %add_bitcast_fusion.own), channel_id=1, source_target_pairs={{0,4},{4,0},{8,12},{12,8},{16,20},{20,16},{24,28},{28,24},{1,5},{5... | collective-permute-start | bytes 1544 | tf_op jit(solution)/shard_map/ppermute | solution.py:39
  3.6 5.3 %collective-permute-start.3 = (s32[2,128]{1,0:T(2,128)S(1)}, s32[2,128]{1,0:T(2,128)S(1)}, u32[]{:S(2)}, u32[]{:S(2)}) collective-permute-start(s32[2,128]{1,0:T(2,128)S(1)} %shard_map.85.refs_0_), channel_id=1, source_target_pairs={{0,24},{4,28},{8,16},{12,20},{16,8},{20,12},{24,0},{28,4},{1,25},{... | collective-permute-start | bytes 3080 | tf_op jit(solution)/shard_map/ppermute | solution.py:51
  7.3 3.6 %collective-permute-start.2 = (s32[2,128]{1,0:T(2,128)S(1)}, s32[2,128]{1,0:T(2,128)S(1)}, u32[]{:S(2)}, u32[]{:S(2)}) collective-permute-start(s32[2,128]{1,0:T(2,128)S(1)} %shard_map.85.refs_0_), channel_id=1, source_target_pairs={{0,16},{4,12},{8,24},{12,4},{16,0},{20,28},{24,8},{28,20},{1,17},{... | collective-permute-start | bytes 3080 | tf_op jit(solution)/shard_map/ppermute | solution.py:51
  7.8 3.6 %collective-permute-start.1 = (s32[2,128]{1,0:T(2,128)S(1)}, s32[2,128]{1,0:T(2,128)S(1)}, u32[]{:S(2)}, u32[]{:S(2)}) collective-permute-start(s32[2,128]{1,0:T(2,128)S(1)} %shard_map.85.refs_0_), channel_id=1, source_target_pairs={{0,8},{4,20},{8,0},{12,28},{16,24},{20,4},{24,16},{28,12},{1,9},{5... | collective-permute-start | bytes 3080 | tf_op jit(solution)/shard_map/ppermute | solution.py:51
  14.7 2.7 %collective-permute-start.11 = (bf16[4,8,128,128]{3,2,1,0:T(8,128)(2,1)S(1)}, bf16[4,8,128,128]{3,2,1,0:T(8,128)(2,1)S(1)}, u32[]{:S(2)}, u32[]{:S(2)}) collective-permute-start(bf16[4,8,128,128]{3,2,1,0:T(8,128)(2,1)S(1)} %get-tuple-element.20), channel_id=1, source_target_pairs={{0,4},{4,0},{8,12},{12,8},{16,20},{20,16},{24,28},{28,24},{1,5},{5... | collective-permute-start | bytes 3145736 | tf_op jit(solution)/shard_map/ppermute | solution.py:39
  17.5 1.8 %copy-start.1 = (bf16[8,128,128]{2,1,0:T(8,128)(2,1)S(1)}, bf16[8,128,128]{2,1,0:T(8,128)(2,1)}, u32[]{:S(2)}) copy-start(bf16[8,128,128]{2,1,0:T(8,128)(2,1)} %refs_0_.1) | copy-start | bytes 786436
  17.6 14.9 %collective-permute-start.12 = (bf16[2,8,128,128]{3,2,1,0:T(8,128)(2,1)S(1)}, bf16[2,8,128,128]{3,2,1,0:T(8,128)(2,1)S(1)}, u32[]{:S(2)}, u32[]{:S(2)}) collective-permute-start(bf16[2,8,128,128]{3,2,1,0:T(8,128)(2,1)S(1)} %get-tuple-element.22), channel_id=1, source_target_pairs={{0,16},{4,12},{8,24},{12,4},{16,0},{20,28},{24,8},{28,20},{1,17},{... | collective-permute-start | bytes 1572872 | tf_op jit(solution)/shard_map/ppermute | solution.py:51
  19.2 13.3 %collective-permute-start.7 = (bf16[8,128,128]{2,1,0:T(8,128)(2,1)S(1)}, bf16[8,128,128]{2,1,0:T(8,128)(2,1)S(1)}, u32[]{:S(2)}, u32[]{:S(2)}) collective-permute-start(bf16[8,128,128]{2,1,0:T(8,128)(2,1)S(1)} %copy-done.1), channel_id=1, source_target_pairs={{0,16},{4,12},{8,24},{12,4},{16,0},{20,28},{24,8},{28,20},{1,17},{... | collective-permute-start | bytes 786440 | tf_op jit(solution)/shard_map/ppermute | solution.py:51
  19.9 18.9 %collective-permute-start.5 = (bf16[8,128,128]{2,1,0:T(8,128)(2,1)S(1)}, bf16[8,128,128]{2,1,0:T(8,128)(2,1)S(1)}, u32[]{:S(2)}, u32[]{:S(2)}) collective-permute-start(bf16[8,128,128]{2,1,0:T(8,128)(2,1)S(1)} %copy-done.1), channel_id=1, source_target_pairs={{0,8},{4,20},{8,0},{12,28},{16,24},{20,4},{24,16},{28,12},{1,9},{5... | collective-permute-start | bytes 786440 | tf_op jit(solution)/shard_map/ppermute | solution.py:51
  32.5 6.4 %collective-permute-start.9 = (bf16[8,128,128]{2,1,0:T(8,128)(2,1)S(1)}, bf16[8,128,128]{2,1,0:T(8,128)(2,1)S(1)}, u32[]{:S(2)}, u32[]{:S(2)}) collective-permute-start(bf16[8,128,128]{2,1,0:T(8,128)(2,1)S(1)} %collective-permute-done.7.refs_4_), channel_id=1, source_target_pairs={{0,8},{4,20},{8,0},{12,28},{16,24},{20,4},{24,16},{28,12},{1,9},{5... | collective-permute-start | bytes 786440 | tf_op jit(solution)/shard_map/ppermute | solution.py:51
  32.7 9.0 %collective-permute-start.13 = (bf16[1,8,128,128]{3,2,1,0:T(8,128)(2,1)S(1)}, bf16[1,8,128,128]{3,2,1,0:T(8,128)(2,1)S(1)}, u32[]{:S(2)}, u32[]{:S(2)}) collective-permute-start(bf16[1,8,128,128]{3,2,1,0:T(8,128)(2,1)S(1)} %get-tuple-element.24), channel_id=1, source_target_pairs={{0,8},{4,20},{8,0},{12,28},{16,24},{20,4},{24,16},{28,12},{1,9},{5... | collective-permute-start | bytes 786440 | tf_op jit(solution)/shard_map/ppermute | solution.py:51
  34.7 8.7 %collective-permute-start.4 = (bf16[8,128,128]{2,1,0:T(8,128)(2,1)S(1)}, bf16[8,128,128]{2,1,0:T(8,128)(2,1)S(1)}, u32[]{:S(2)}, u32[]{:S(2)}) collective-permute-start(bf16[8,128,128]{2,1,0:T(8,128)(2,1)S(1)} %copy-done.1), channel_id=1, source_target_pairs={{0,4},{4,0},{8,12},{12,8},{16,20},{20,16},{24,28},{28,24},{1,5},{5... | collective-permute-start | bytes 786440 | tf_op jit(solution)/shard_map/ppermute | solution.py:39
  38.3 7.9 %collective-permute-start.8 = (bf16[8,128,128]{2,1,0:T(8,128)(2,1)S(1)}, bf16[8,128,128]{2,1,0:T(8,128)(2,1)S(1)}, u32[]{:S(2)}, u32[]{:S(2)}) collective-permute-start(bf16[8,128,128]{2,1,0:T(8,128)(2,1)S(1)} %collective-permute-done.7.refs_4_), channel_id=1, source_target_pairs={{0,4},{4,0},{8,12},{12,8},{16,20},{20,16},{24,28},{28,24},{1,5},{5... | collective-permute-start | bytes 786440 | tf_op jit(solution)/shard_map/ppermute | solution.py:39
  38.9 7.1 %collective-permute-start.6 = (bf16[8,128,128]{2,1,0:T(8,128)(2,1)S(1)}, bf16[8,128,128]{2,1,0:T(8,128)(2,1)S(1)}, u32[]{:S(2)}, u32[]{:S(2)}) collective-permute-start(bf16[8,128,128]{2,1,0:T(8,128)(2,1)S(1)} %collective-permute-done.5.refs_2_), channel_id=1, source_target_pairs={{0,4},{4,0},{8,12},{12,8},{16,20},{20,16},{24,28},{28,24},{1,5},{5... | collective-permute-start | bytes 786440 | tf_op jit(solution)/shard_map/ppermute | solution.py:39
  39.0 7.2 %collective-permute-start.10 = (bf16[8,128,128]{2,1,0:T(8,128)(2,1)S(1)}, bf16[8,128,128]{2,1,0:T(8,128)(2,1)S(1)}, u32[]{:S(2)}, u32[]{:S(2)}) collective-permute-start(bf16[8,128,128]{2,1,0:T(8,128)(2,1)S(1)} %collective-permute-done.9.refs_6_), channel_id=1, source_target_pairs={{0,4},{4,0},{8,12},{12,8},{16,20},{20,16},{24,28},{28,24},{1,5},{5... | collective-permute-start | bytes 786440 | tf_op jit(solution)/shard_map/ppermute | solution.py:39
  41.7 9.5 %collective-permute-start.14 = (bf16[2,128,128]{2,1,0:T(8,128)(2,1)S(1)}, bf16[2,128,128]{2,1,0:T(8,128)(2,1)S(1)}, u32[]{:S(2)}, u32[]{:S(2)}) collective-permute-start(bf16[2,128,128]{2,1,0:T(8,128)(2,1)S(1)} %get-tuple-element.26), channel_id=1, source_target_pairs={{0,1},{1,0},{2,3},{3,2},{4,5},{5,4},{6,7},{7,6},{8,9},{9,8},{10,11... | collective-permute-start | bytes 196616 | tf_op jit(solution)/shard_map/ppermute | solution.py:39
  43.4 7.8 %collective-permute-start.15 = (bf16[2,128,128]{2,1,0:T(8,128)(2,1)S(1)}, bf16[2,128,128]{2,1,0:T(8,128)(2,1)S(1)}, u32[]{:S(2)}, u32[]{:S(2)}) collective-permute-start(bf16[2,128,128]{2,1,0:T(8,128)(2,1)S(1)} %get-tuple-element.27), channel_id=1, source_target_pairs={{0,2},{1,3},{2,0},{3,1},{4,6},{5,7},{6,4},{7,5},{8,10},{9,11},{10,... | collective-permute-start | bytes 196616 | tf_op jit(solution)/shard_map/ppermute | solution.py:39
  46.0 6.1 %collective-permute-start.16 = (bf16[2,128,128]{2,1,0:T(8,128)(2,1)S(1)}, bf16[2,128,128]{2,1,0:T(8,128)(2,1)S(1)}, u32[]{:S(2)}, u32[]{:S(2)}) collective-permute-start(bf16[2,128,128]{2,1,0:T(8,128)(2,1)S(1)} %get-tuple-element.28), channel_id=1, source_target_pairs={{0,3},{1,2},{2,1},{3,0},{4,7},{5,6},{6,5},{7,4},{8,11},{9,10},{10,... | collective-permute-start | bytes 196616 | tf_op jit(solution)/shard_map/ppermute | solution.py:39
  51.2 1.5 %copy-start.2 = (bf16[64,128,128]{2,1,0:T(8,128)(2,1)}, bf16[64,128,128]{2,1,0:T(8,128)(2,1)S(1)}, u32[]{:S(2)}) copy-start(bf16[64,128,128]{2,1,0:T(8,128)(2,1)S(1)} %get-tuple-element.18.refs_0_) | copy-start | bytes 6291460
  52.7 17.5 %collective-permute-start.19 = (bf16[2,128,128]{2,1,0:T(8,128)(2,1)S(1)}, bf16[2,128,128]{2,1,0:T(8,128)(2,1)S(1)}, u32[]{:S(2)}, u32[]{:S(2)}) collective-permute-start(bf16[2,128,128]{2,1,0:T(8,128)(2,1)S(1)} %get-tuple-element.30.refs_5_), channel_id=1, source_target_pairs={{0,3},{1,2},{2,1},{3,0},{4,7},{5,6},{6,5},{7,4},{8,11},{9,10},{10,... | collective-permute-start | bytes 196616 | tf_op jit(solution)/shard_map/ppermute | solution.py:39
  56.1 14.1 %collective-permute-start.18 = (bf16[2,128,128]{2,1,0:T(8,128)(2,1)S(1)}, bf16[2,128,128]{2,1,0:T(8,128)(2,1)S(1)}, u32[]{:S(2)}, u32[]{:S(2)}) collective-permute-start(bf16[2,128,128]{2,1,0:T(8,128)(2,1)S(1)} %get-tuple-element.30.refs_5_), channel_id=1, source_target_pairs={{0,2},{1,3},{2,0},{3,1},{4,6},{5,7},{6,4},{7,5},{8,10},{9,11},{10,... | collective-permute-start | bytes 196616 | tf_op jit(solution)/shard_map/ppermute | solution.py:39
  56.1 14.1 %collective-permute-start.17 = (bf16[2,128,128]{2,1,0:T(8,128)(2,1)S(1)}, bf16[2,128,128]{2,1,0:T(8,128)(2,1)S(1)}, u32[]{:S(2)}, u32[]{:S(2)}) collective-permute-start(bf16[2,128,128]{2,1,0:T(8,128)(2,1)S(1)} %get-tuple-element.30.refs_5_), channel_id=1, source_target_pairs={{0,1},{1,0},{2,3},{3,2},{4,5},{5,4},{6,7},{7,6},{8,9},{9,8},{10,11... | collective-permute-start | bytes 196616 | tf_op jit(solution)/shard_map/ppermute | solution.py:39
  57.1 13.1 %all-to-all-start = ((f32[32,1,128]{2,1,0:T(1,128)}), f32[32,1,128]{2,1,0:T(1,128)S(1)}, u32[]{:S(2)}, u32[]{:S(2)}) async-start(f32[32,1,128]{2,1,0:T(1,128)} %get-tuple-element.29), calls=%async_computation | async-start | bytes 32768 | tf_op jit(solution)/shard_map/all_to_all | solution.py:339
  61.8 1.6 %copy-start.3 = (bf16[64,128,128]{2,1,0:T(8,128)(2,1)S(1)}, bf16[64,128,128]{2,1,0:T(8,128)(2,1)}, u32[]{:S(2)}) copy-start(bf16[64,128,128]{2,1,0:T(8,128)(2,1)} %copy-done.2) | copy-start | bytes 6291460
